TPU v7x, 32 devices: a whole 2x2x4 slice. The times are simulated.
32 devices in a mesh: fsdp: 16 (over z, y, core), tp: 2 (over x).
Axes of the slice: x: 2, y: 2, z: 4, core: 2. Of those that a mesh axis runs over, the one named last changes fastest.
Arguments:
- inputs: bfloat16 [2, 16384, 768], P(None, ('fsdp', 'tp')), may hold values from -60 to 60
- image_ids: int32 [2, 16384], P(None, ('fsdp', 'tp')), may hold values from 0 to 127, never falling along the last dimension, each value on 1 to 256 neighbouring positions
- cotangent: bfloat16 [2, 16384, 768], P(None, ('fsdp', 'tp')), may hold values from -36 to 36
- norm1_gain: float32 [768], replicated, may hold values from 0.25 to 1.75
- norm1_bias: float32 [768], replicated, may hold values from -3 to 3
- qkv_weight: bfloat16 [768, 3, 768], P('fsdp', None, 'tp'), may hold values from -0.21875 to 0.21875
- qkv_bias: float32 [3, 768], P(None, 'tp'), may hold values from -3 to 3
- query_gain: float32 [64], replicated, may hold values from 0.25 to 1.75
- query_bias: float32 [64], replicated, may hold values from -3 to 3
- key_gain: float32 [64], replicated, may hold values from 0.25 to 1.75
- out_weight: bfloat16 [768, 768], P('tp', 'fsdp'), may hold values from -0.875 to 0.875
- out_bias: float32 [768], replicated, may hold values from -3 to 3
- norm2_gain: float32 [768], replicated, may hold values from 0.25 to 1.75
- norm2_bias: float32 [768], replicated, may hold values from -3 to 3
- up_weight: bfloat16 [768, 3072], P('fsdp', 'tp'), may hold values from -0.21875 to 0.21875
- up_bias: float32 [3072], P('tp'), may hold values from -3 to 3
- down_weight: bfloat16 [3072, 768], P('tp', 'fsdp'), may hold values from -0.109375 to 0.109375
- down_bias: float32 [768], replicated, may hold values from -3 to 3
Outputs:
- output: bfloat16 [2, 16384, 768], P(None, ('fsdp', 'tp'))
- input_grad: float32 [2, 16384, 768], P(None, ('fsdp', 'tp'))
- norm1_gain_grad: float32 [768], replicated
- norm1_bias_grad: float32 [768], replicated
- qkv_weight_grad: float32 [768, 3, 768], P('fsdp', None, 'tp')
- qkv_bias_grad: float32 [3, 768], P(None, 'tp')
- query_gain_grad: float32 [64], replicated
- query_bias_grad: float32 [64], replicated
- key_gain_grad: float32 [64], replicated
- out_weight_grad: float32 [768, 768], P('tp', 'fsdp')
- out_bias_grad: float32 [768], replicated
- norm2_gain_grad: float32 [768], replicated
- norm2_bias_grad: float32 [768], replicated
- up_weight_grad: float32 [768, 3072], P('fsdp', 'tp')
- up_bias_grad: float32 [3072], P('tp')
- down_weight_grad: float32 [3072, 768], P('tp', 'fsdp')
- down_bias_grad: float32 [768], replicated
Inputs may be any that keep to these rules, and one draw needn't show every extreme that they name: `image_ids`: along each micro-batch's row of 16384 tokens the image ids never fall; every image has 1 to 256 tokens, and one has exactly 256.
All inputs are finite; a program needn't handle non-finite values.
Results may differ from a plain program's by a relative error of at most 0.01.
Values may be sent and summed in bfloat16 or wider, within the bound.
A program may use at most 192 MiB of HBM per device.

v0:
```python
from functools import partial

import jax
import jax.numpy as jnp
from jax import lax
from jax.sharding import PartitionSpec as P

LEN = 1024


EPSILON = 1e-06


def norm_parts(values):
    average = jnp.mean(values, axis=-1, keepdims=True)
    centred = values - average
    spread = jnp.mean(centred * centred, axis=-1, keepdims=True)
    scaled = lax.rsqrt(spread + EPSILON)
    return (centred * scaled, scaled)


def norm_back(grad_out, unit, scaled, gain):
    grad_unit = grad_out * gain
    first = jnp.mean(grad_unit, axis=-1, keepdims=True)
    second = jnp.mean(grad_unit * unit, axis=-1, keepdims=True)
    return scaled * (grad_unit - first - unit * second)


def masked_scores(query_block, query_ids, keys, key_ids, scale):
    scores = (
        jnp.einsum("qhd,khd->hqk", query_block, keys, preferred_element_type=jnp.float32) * scale
    )
    same = (query_ids[:, None] == key_ids[None, :])[None]
    return jnp.where(same, scores, -1e30)


def attend_block(query_block, query_ids, keys, values, key_ids, scale):
    masked = masked_scores(query_block, query_ids, keys, key_ids, scale)
    highest = jnp.max(masked, axis=-1, keepdims=True)
    total = jnp.sum(jnp.exp(masked - highest), axis=-1, keepdims=True)
    log_total = highest + jnp.log(total)
    weights = jnp.exp(masked - log_total).astype(jnp.bfloat16)
    mixed = jnp.einsum("hqk,khd->qhd", weights, values, preferred_element_type=jnp.float32)
    return (mixed, log_total)


def attend_back(query_block, query_ids, keys, values, key_ids, log_total, grad_block, scale):
    masked = masked_scores(query_block, query_ids, keys, key_ids, scale)
    weights = jnp.exp(masked - log_total)
    rounded = weights.astype(jnp.bfloat16)
    grad_weights = jnp.einsum(
        "qhd,khd->hqk", grad_block, values, preferred_element_type=jnp.float32
    )
    inner = jnp.sum(grad_weights * weights, axis=-1, keepdims=True)
    grad_scores = (weights * (grad_weights - inner)).astype(jnp.bfloat16)
    grad_query = (
        jnp.einsum("hqk,khd->qhd", grad_scores, keys, preferred_element_type=jnp.float32) * scale
    )
    grad_keys = (
        jnp.einsum("hqk,qhd->khd", grad_scores, query_block, preferred_element_type=jnp.float32)
        * scale
    )
    grad_values = jnp.einsum(
        "hqk,qhd->khd", rounded, grad_block, preferred_element_type=jnp.float32
    )
    return (grad_query, grad_keys, grad_values)


def sequence_forward(pieces, scale):
    queries, keys, values, seq_ids = pieces
    length, heads, depth = queries.shape
    block = min(512, length)
    count = length // block

    def one_block(part):
        return attend_block(part[0], part[1], keys, values, seq_ids, scale)

    mixed, log_total = lax.map(
        one_block, (queries.reshape(count, block, heads, depth), seq_ids.reshape(count, block))
    )
    return (mixed.reshape(length, heads, depth), log_total)


def sequence_back(pieces, scale):
    queries, keys, values, seq_ids, log_total, grad_mixed = pieces
    length, heads, depth = queries.shape
    block = min(512, length)
    count = length // block

    def one_block(carry, part):
        query_block, query_ids, log_block, grad_block = part
        grad_query, grad_keys, grad_values = attend_back(
            query_block, query_ids, keys, values, seq_ids, log_block, grad_block, scale
        )
        return ((carry[0] + grad_keys, carry[1] + grad_values), grad_query)

    zeros = jnp.zeros(keys.shape, jnp.float32)
    parts = (
        queries.reshape(count, block, heads, depth),
        seq_ids.reshape(count, block),
        log_total,
        grad_mixed.reshape(count, block, heads, depth),
    )
    (grad_keys, grad_values), grad_queries = lax.scan(one_block, (zeros, zeros), parts)
    return (grad_queries.reshape(length, heads, depth), grad_keys, grad_values)


def add_tuples(first, second):
    if first is None:
        return second
    return tuple((a + b for a, b in zip(first, second)))


def on_device(
    inputs,
    image_ids,
    cotangent,
    norm1_gain,
    norm1_bias,
    qkv_weight,
    qkv_bias,
    query_gain,
    query_bias,
    key_gain,
    out_weight,
    out_bias,
    norm2_gain,
    norm2_bias,
    up_weight,
    up_bias,
    down_weight,
    down_bias,
):
    batches, rows_here, width = inputs.shape
    head_dim = query_gain.shape[0]
    local_width = qkv_weight.shape[2]
    local_heads = local_width // head_dim
    local_hidden = up_weight.shape[1]
    group_rows = rows_here * lax.axis_size("tp")
    seq_count = group_rows // LEN
    scale = head_dim ** (-0.5)
    seq_shape = (seq_count, LEN, local_heads, head_dim)
    grad_qkv_bias = jnp.zeros((3, local_width), jnp.float32)
    grad_up_bias = jnp.zeros((local_hidden,), jnp.float32)
    grad_out_bias = jnp.zeros((width,), jnp.float32)
    grad_down_bias = jnp.zeros((width,), jnp.float32)
    grad_gain_one = jnp.zeros((width,), jnp.float32)
    grad_shift_one = jnp.zeros((width,), jnp.float32)
    grad_gain_two = jnp.zeros((width,), jnp.float32)
    grad_shift_two = jnp.zeros((width,), jnp.float32)
    grad_gain_query = jnp.zeros((head_dim,), jnp.float32)
    grad_shift_query = jnp.zeros((head_dim,), jnp.float32)
    grad_gain_key = jnp.zeros((head_dim,), jnp.float32)
    totals = None
    outputs = []
    in_grads = []
    for batch in range(batches):
        full_qkv, full_out, full_up, full_down = (
            lax.all_gather(qkv_weight, "fsdp", axis=0, tiled=True),
            lax.all_gather(out_weight, "fsdp", axis=1, tiled=True),
            lax.all_gather(up_weight, "fsdp", axis=0, tiled=True),
            lax.all_gather(down_weight, "fsdp", axis=1, tiled=True),
        )
        qkv_matrix = full_qkv.reshape(width, 3 * local_width)
        tokens_in = inputs[batch].astype(jnp.float32)
        unit_one, scaled_one = norm_parts(tokens_in)
        normed1 = (unit_one * norm1_gain + norm1_bias).astype(jnp.bfloat16)
        rows_one, group_ids = (
            lax.all_gather(normed1, "tp", axis=0, tiled=True),
            lax.all_gather(image_ids[batch], "tp", axis=0, tiled=True),
        )
        project = jnp.dot(rows_one, qkv_matrix, preferred_element_type=jnp.float32)
        project = (project + qkv_bias.reshape(3 * local_width)).reshape(
            group_rows, 3, local_heads, head_dim
        )
        query_unit, query_scaled = norm_parts(project[:, 0])
        key_unit, key_scaled = norm_parts(project[:, 1])
        queries = (query_unit * query_gain + query_bias).astype(jnp.bfloat16)
        keys = (key_unit * key_gain).astype(jnp.bfloat16)
        values = project[:, 2].astype(jnp.bfloat16)
        seq_ids = group_ids.reshape(seq_count, LEN)
        mixed, log_total = lax.map(
            partial(sequence_forward, scale=scale),
            (
                queries.reshape(seq_shape),
                keys.reshape(seq_shape),
                values.reshape(seq_shape),
                seq_ids,
            ),
        )
        mixed_low = mixed.reshape(group_rows, local_width).astype(jnp.bfloat16)
        attended = lax.psum_scatter(
            jnp.dot(mixed_low, full_out, preferred_element_type=jnp.float32).astype(jnp.bfloat16),
            "tp",
            scatter_dimension=0,
            tiled=True,
        ).astype(jnp.float32)
        resid = tokens_in + attended + out_bias
        unit_two, scaled_two = norm_parts(resid)
        normed2 = (unit_two * norm2_gain + norm2_bias).astype(jnp.bfloat16)
        rows_two = lax.all_gather(normed2, "tp", axis=0, tiled=True)
        preact = jnp.dot(rows_two, full_up, preferred_element_type=jnp.float32) + up_bias
        hidden, gelu_back = jax.vjp(partial(jax.nn.gelu, approximate=False), preact)
        hidden_low = hidden.astype(jnp.bfloat16)
        down_piece = lax.slice_in_dim(hidden_low, 0, rows_here * lax.axis_size("tp"), axis=0)
        branch = lax.psum_scatter(
            jnp.dot(down_piece, full_down, preferred_element_type=jnp.float32).astype(jnp.bfloat16),
            "tp",
            scatter_dimension=0,
            tiled=True,
        ).astype(jnp.float32)
        outputs.append((resid + branch + down_bias).astype(jnp.bfloat16))
        full_qkv, full_out, full_up, full_down = (
            lax.all_gather(qkv_weight, "fsdp", axis=0, tiled=True),
            lax.all_gather(out_weight, "fsdp", axis=1, tiled=True),
            lax.all_gather(up_weight, "fsdp", axis=0, tiled=True),
            lax.all_gather(down_weight, "fsdp", axis=1, tiled=True),
        )
        qkv_matrix = full_qkv.reshape(width, 3 * local_width)
        grad_y = cotangent[batch].astype(jnp.float32)
        grad_down_bias = grad_down_bias + jnp.sum(grad_y, axis=0)
        grad_out_rows = lax.all_gather(grad_y.astype(jnp.bfloat16), "tp", axis=0, tiled=True)
        term_down = jnp.einsum(
            "gf,gd->fd", hidden_low, grad_out_rows, preferred_element_type=jnp.float32
        )
        grad_hidden = jnp.einsum(
            "gd,fd->gf", grad_out_rows, full_down, preferred_element_type=jnp.float32
        )
        grad_preact = gelu_back(grad_hidden)[0].astype(jnp.bfloat16)
        grad_up_bias = grad_up_bias + jnp.sum(grad_preact.astype(jnp.float32), axis=0)
        term_up = jnp.einsum("gd,gf->df", rows_two, grad_preact, preferred_element_type=jnp.float32)
        grad_normed2 = lax.psum_scatter(
            jnp.einsum(
                "gf,df->gd", grad_preact, full_up, preferred_element_type=jnp.float32
            ).astype(jnp.bfloat16),
            "tp",
            scatter_dimension=0,
            tiled=True,
        ).astype(jnp.float32)
        grad_gain_two = grad_gain_two + jnp.sum(grad_normed2 * unit_two, axis=0)
        grad_shift_two = grad_shift_two + jnp.sum(grad_normed2, axis=0)
        grad_resid = grad_y + norm_back(grad_normed2, unit_two, scaled_two, norm2_gain)
        grad_out_bias = grad_out_bias + jnp.sum(grad_resid, axis=0)
        grad_attn_rows = lax.all_gather(grad_resid.astype(jnp.bfloat16), "tp", axis=0, tiled=True)
        term_out = jnp.einsum(
            "gc,gd->cd", mixed_low, grad_attn_rows, preferred_element_type=jnp.float32
        )
        grad_mixed = jnp.einsum(
            "gd,cd->gc", grad_attn_rows, full_out, preferred_element_type=jnp.float32
        ).astype(jnp.bfloat16)
        grad_queries, grad_keys, grad_values = lax.map(
            partial(sequence_back, scale=scale),
            (
                queries.reshape(seq_shape),
                keys.reshape(seq_shape),
                values.reshape(seq_shape),
                seq_ids,
                log_total,
                grad_mixed.reshape(seq_shape),
            ),
        )
        grad_queries = grad_queries.reshape(group_rows, local_heads, head_dim)
        grad_keys = grad_keys.reshape(group_rows, local_heads, head_dim)
        grad_values = grad_values.reshape(group_rows, local_heads, head_dim)
        grad_gain_query = grad_gain_query + jnp.sum(grad_queries * query_unit, axis=(0, 1))
        grad_shift_query = grad_shift_query + jnp.sum(grad_queries, axis=(0, 1))
        grad_gain_key = grad_gain_key + jnp.sum(grad_keys * key_unit, axis=(0, 1))
        grad_query_raw = norm_back(grad_queries, query_unit, query_scaled, query_gain)
        grad_key_raw = norm_back(grad_keys, key_unit, key_scaled, key_gain)
        grad_project = jnp.stack([grad_query_raw, grad_key_raw, grad_values], axis=1)
        grad_project = grad_project.reshape(group_rows, 3 * local_width).astype(jnp.bfloat16)
        grad_qkv_bias = grad_qkv_bias + jnp.sum(grad_project.astype(jnp.float32), axis=0).reshape(
            3, local_width
        )
        term_qkv = jnp.einsum(
            "gd,gc->dc", rows_one, grad_project, preferred_element_type=jnp.float32
        ).reshape(width, 3, local_width)
        grad_normed1 = lax.psum_scatter(
            jnp.einsum(
                "gc,dc->gd", grad_project, qkv_matrix, preferred_element_type=jnp.float32
            ).astype(jnp.bfloat16),
            "tp",
            scatter_dimension=0,
            tiled=True,
        ).astype(jnp.float32)
        grad_gain_one = grad_gain_one + jnp.sum(grad_normed1 * unit_one, axis=0)
        grad_shift_one = grad_shift_one + jnp.sum(grad_normed1, axis=0)
        in_grads.append(grad_resid + norm_back(grad_normed1, unit_one, scaled_one, norm1_gain))
        terms = (term_qkv, term_out, term_up, term_down)
        totals = add_tuples(totals, terms)
    qkv_weight_grad, out_weight_grad, up_weight_grad, down_weight_grad = (
        lax.psum_scatter(totals[0], "fsdp", scatter_dimension=0, tiled=True),
        lax.psum_scatter(totals[1], "fsdp", scatter_dimension=1, tiled=True),
        lax.psum_scatter(totals[2], "fsdp", scatter_dimension=0, tiled=True),
        lax.psum_scatter(totals[3], "fsdp", scatter_dimension=1, tiled=True),
    )
    (
        qkv_bias_grad,
        up_bias_grad,
        grad_out_bias,
        grad_down_bias,
        grad_gain_one,
        grad_shift_one,
        grad_gain_two,
        grad_shift_two,
        grad_gain_query,
        grad_shift_query,
        grad_gain_key,
    ) = lax.psum(
        (
            grad_qkv_bias,
            grad_up_bias,
            grad_out_bias,
            grad_down_bias,
            grad_gain_one,
            grad_shift_one,
            grad_gain_two,
            grad_shift_two,
            grad_gain_query,
            grad_shift_query,
            grad_gain_key,
        ),
        "fsdp",
    )
    (
        out_bias_grad,
        down_bias_grad,
        norm1_gain_grad,
        norm1_bias_grad,
        norm2_gain_grad,
        norm2_bias_grad,
        query_gain_grad,
        query_bias_grad,
        key_gain_grad,
    ) = lax.psum(
        (
            grad_out_bias,
            grad_down_bias,
            grad_gain_one,
            grad_shift_one,
            grad_gain_two,
            grad_shift_two,
            grad_gain_query,
            grad_shift_query,
            grad_gain_key,
        ),
        "tp",
    )
    return (
        jnp.stack(outputs),
        jnp.stack(in_grads),
        norm1_gain_grad,
        norm1_bias_grad,
        qkv_weight_grad,
        qkv_bias_grad,
        query_gain_grad,
        query_bias_grad,
        key_gain_grad,
        out_weight_grad,
        out_bias_grad,
        norm2_gain_grad,
        norm2_bias_grad,
        up_weight_grad,
        up_bias_grad,
        down_weight_grad,
        down_bias_grad,
    )


def solution(mesh):
    placed = (
        P(None, ("fsdp", "tp"), None),
        P(None, ("fsdp", "tp")),
        P(None, ("fsdp", "tp"), None),
        P(),
        P(),
        P("fsdp", None, "tp"),
        P(None, "tp"),
        P(),
        P(),
        P(),
        P("tp", "fsdp"),
        P(),
        P(),
        P(),
        P("fsdp", "tp"),
        P("tp"),
        P("tp", "fsdp"),
        P(),
    )
    return jax.shard_map(
        on_device,
        mesh=mesh,
        in_specs=placed,
        out_specs=(
            P(None, ("fsdp", "tp"), None),
            P(None, ("fsdp", "tp"), None),
            P(),
            P(),
            P("fsdp", None, "tp"),
            P(None, "tp"),
            P(),
            P(),
            P(),
            P("tp", "fsdp"),
            P(),
            P(),
            P(),
            P("fsdp", "tp"),
            P("tp"),
            P("tp", "fsdp"),
            P(),
        ),
        check_vma=False,
    )
```

profile of v0, /device:TPU:0, one launch (start us, length us, event | category | flops | bytes accessed | tf_op | source)
XLA Modules:
  0.0 1137.1 jit_solution(17100581439481794679)
XLA Ops:
  26.4 25.8 %all_gather.57 = bf16[384,768]{0,1:T(8,128)(2,1)} all-gather(bf16[384,48]{0,1:T(8,128)(2,1)S(1)} %copy-done.100), channel_id=1, replica_groups=mesh['fsdp'=16,'tp'=2] {'fsdp'}, dimensions={1}, use_global_device_ids=true | all-gather | bytes 626688 | tf_op jit(solution)/shard_map/all_gather | solution.py:160
  57.5 25.8 %all-gather.16.cloned.1.call-done = bf16[1024,768]{1,0:T(8,128)(2,1)} async-done(((bf16[512,768]{1,0:T(8,128)(2,1)}), bf16[1024,768]{1,0:T(8,128)(2,1)}) %all-gather.16.cloned.1.call-update) | async-done | bytes 1572880 | tf_op jit(solution)/shard_map/all_gather | solution.py:169
  83.3 5.8 convolution_add_fusion.1
  89.1 6.1 copy.68
  95.3 17.4 %all-gather.26.cloned.1.call-done = bf16[1024,768]{1,0:T(8,128)(2,1)} async-done(((bf16[512,768]{1,0:T(8,128)(2,1)}), bf16[1024,768]{1,0:T(8,128)(2,1)}) %all-gather.26.cloned.1.call-update) | async-done | bytes 1572880 | tf_op jit(solution)/shard_map/all_gather | solution.py:169
  112.7 5.8 convolution_add_fusion
  118.5 6.1 copy.71
  153.8 32.7 %while.95 = (s32[]{:T(128)}, bf16[2,512,6,64]{1,3,2,0:T(8,128)(2,1)}, f32[2,6,512,1]{2,1,3,0:T(8,128)S(1)}, s32[2,512]{1,0:T(2,128)S(1)}, s32[1024]{0:T(1024)S(1...) while((s32[]{:T(128)}, ...), condition=%wide.region_23.24_spmd, body=%wide.region_20.23_spmd.sunk | while | flops 840430592 | bytes 102496472 | solution.py:78
  161.5 7.8 fusion.267
  177.8 7.8 fusion.267
  193.7 30.9 %while.94 = (s32[]{:T(128)}, bf16[2,512,6,64]{1,3,2,0:T(8,128)(2,1)S(1)}, f32[2,6,512,1]{2,1,3,0:T(8,128)S(1)}, s32[2,512]{1,0:T(2,128)S(1)}, s32[1024]{0:T(1024...) while((s32[]{:T(128)}, ...), condition=%wide.region_9.10_spmd, body=%wide.region_6.9_spmd.sunk | while | flops 840430592 | bytes 93059200 | solution.py:78
  201.6 7.8 fusion.263
  216.8 7.8 fusion.263
  229.0 25.6 %reduce-scatter.13.cloned.1.call-done = bf16[512,768]{1,0:T(8,128)(2,1)} async-done(((bf16[1024,768]{1,0:T(8,128)(2,1)}), bf16[512,768]{1,0:T(8,128)(2,1)}) %reduce-scatter.13.cloned.1.call-update) | async-done | bytes 786448 | tf_op jit(solution)/shard_map/reduce_scatter | solution.py:192
  264.7 34.4 %all-gather.22.cloned.1.call-done = bf16[768,1536]{1,0:T(8,128)(2,1)} async-done(((bf16[48,1536]{1,0:T(8,128)(2,1)}), bf16[768,1536]{1,0:T(8,128)(2,1)}) %all-gather.22.cloned.1.call-update) | async-done | bytes 2359312 | tf_op jit(solution)/shard_map/all_gather | solution.py:161
  299.2 28.0 %all-gather.28.cloned.1.call-done = bf16[1024,768]{1,0:T(8,128)(2,1)} async-done(((bf16[512,768]{1,0:T(8,128)(2,1)}), bf16[1024,768]{1,0:T(8,128)(2,1)}) %all-gather.28.cloned.1.call-update) | async-done | bytes 1572880 | tf_op jit(solution)/shard_map/all_gather | solution.py:201
  327.2 7.3 fusion.171
  334.5 22.0 %all-gather.20.cloned.1.call-done = bf16[1024,768]{1,0:T(8,128)(2,1)} async-done(((bf16[512,768]{1,0:T(8,128)(2,1)}), bf16[1024,768]{1,0:T(8,128)(2,1)}) %all-gather.20.cloned.1.call-update) | async-done | bytes 1572880 | tf_op jit(solution)/shard_map/all_gather | solution.py:201
  356.5 32.9 %multiply_convert_fusion.3 = (bf16[1024,1536]{1,0:T(8,128)(2,1)}, f32[1024,1536]{1,0:T(8,128)}, bf16[1024,1536]{1,0:T(8,128)(2,1)}, f32[1024,1536]{1,0:T(8,128)}, f32[1024,1536]{1,0:T(8,128)}) fusion(f32[1536]{0:T(1024)S(1)} %copy-done.129, f32[1024,1536]{1,0:T(8,128)} %fusion.171, bf16[1024,768]{1,0:T(8,128)(2,1)} %all-gather.20.cloned.1.call-done, ...), kind=kOutput, calls=%fused_computation.117 | convolution fusion | flops 2623537152 | bytes 35395584 | tf_op jit(solution)/shard_map/dot_general | solution.py:202
  389.5 40.3 %all-gather.24.cloned.1.call-done = bf16[1536,768]{0,1:T(8,128)(2,1)} async-done(((bf16[1536,48]{0,1:T(8,128)(2,1)}), bf16[1536,768]{0,1:T(8,128)(2,1)}) %all-gather.24.cloned.1.call-update) | async-done | bytes 2359312 | tf_op jit(solution)/shard_map/all_gather | solution.py:162
  429.8 10.9 convert_reduce_fusion
  446.4 10.8 all-gather.34.cloned.1.call-done
  457.3 10.9 convert_reduce_fusion.1
  473.7 6.4 convolution_convert_fusion.7
  480.1 6.5 convolution_convert_fusion.6
  486.7 27.8 %reduce-scatter.21.cloned.1.call-done = bf16[512,768]{1,0:T(8,128)(2,1)} async-done(((bf16[1024,768]{1,0:T(8,128)(2,1)}), bf16[512,768]{1,0:T(8,128)(2,1)}) %reduce-scatter.21.cloned.1.call-update) | async-done | bytes 786448 | tf_op jit(solution)/shard_map/reduce_scatter | solution.py:232
  514.5 28.3 %reduce-scatter.15.cloned.1.call-done = bf16[512,768]{1,0:T(8,128)(2,1)} async-done(((bf16[1024,768]{1,0:T(8,128)(2,1)}), bf16[512,768]{1,0:T(8,128)(2,1)}) %reduce-scatter.15.cloned.1.call-update) | async-done | bytes 786448 | tf_op jit(solution)/shard_map/reduce_scatter | solution.py:206
  542.8 28.3 %reduce-scatter.19.cloned.1.call-done = bf16[512,768]{1,0:T(8,128)(2,1)} async-done(((bf16[1024,768]{1,0:T(8,128)(2,1)}), bf16[512,768]{1,0:T(8,128)(2,1)}) %reduce-scatter.19.cloned.1.call-update) | async-done | bytes 786448 | tf_op jit(solution)/shard_map/reduce_scatter | solution.py:206
  583.5 25.6 %all-gather.32.cloned.1.call-done = bf16[1024,768]{1,0:T(8,128)(2,1)} async-done(((bf16[512,768]{1,0:T(8,128)(2,1)}), bf16[1024,768]{1,0:T(8,128)(2,1)}) %all-gather.32.cloned.1.call-update) | async-done | bytes 1572880 | tf_op jit(solution)/shard_map/all_gather | solution.py:244
  616.9 62.3 %while.97 = (s32[]{:T(128)}, f32[1024,6,64]{0,2,1:T(8,128)}, f32[1024,6,64]{0,2,1:T(8,128)}, f32[2,512,6,64]{1,3,2,0:T(8,128)}, bf16[2,512,6,64]{1,3,2,0:T(8,128...) while((s32[]{:T(128)}, f32[1024,6,64]{0,2,1:T(8,128)}, ...), condition=%wide.region_46.47_spmd.clone, body=%wide.region_44.46_spmd.clone.sunk | while | flops 2063135744 | bytes 211389680 | solution.py:104
  619.6 6.3 multiply_reduce_fusion.21
  636.2 6.4 fusion.289
  649.7 6.3 multiply_reduce_fusion.21
  661.0 5.7 bitcast_add_fusion.10
  666.8 6.4 fusion.289
  673.2 6.0 bitcast_add_fusion.11
  687.1 62.0 %while.96 = (s32[]{:T(128)}, f32[1024,6,64]{0,2,1:T(8,128)}, f32[1024,6,64]{0,2,1:T(8,128)}, f32[2,512,6,64]{1,3,2,0:T(8,128)}, bf16[2,512,6,64]{1,3,2,0:T(8,128...) while((s32[]{:T(128)}, f32[1024,6,64]{0,2,1:T(8,128)}, ...), condition=%wide.region_33.34_spmd.clone, body=%wide.region_31.33_spmd.clone.sunk | while | flops 2063135744 | bytes 211389680 | solution.py:104
  689.5 6.3 multiply_reduce_fusion.20
  706.2 6.4 fusion.278
  719.7 6.3 multiply_reduce_fusion.20
  736.7 6.4 fusion.278
  743.1 6.0 bitcast_add_fusion.9
  749.1 11.6 %multiply_reduce_fusion.5 = (f32[64]{0:T(128)S(1)}, f32[2,512,6]{1,0,2:T(2,128)S(1)}, f32[2,512,6]{1,0,2:T(2,128)S(1)}, f32[2,512,6,64]{1,0,3,2:T(2,128)S(1)}, f...) fusion(f32[2,512,6]{1,0,2:T(2,128)} %copy-done.87, ...), kind=kLoop, calls=%fused_computation.248 | loop fusion | flops 6266752 | bytes 9634560 | tf_op jit(solution)/shard_map/reduce_sum | solution.py:265
  840.8 61.2 %all-reduce = (f32[768]{0:T(1024)S(1)}, f32[768]{0:T(1024)S(1)}, f32[3,384]{1,0:T(4,128)}, f32[64]{0:T(128)S(1)}, f32[64]{0:T(128)S(1)}, /*index=5*/f32[64]{0:T(...) all-reduce(f32[768]{0:T(1024)S(1)} %add.412, ...), channel_id=1, replica_groups=mesh['fsdp'=16,'tp'=2] {'fsdp'}, use_global_device_ids=true, to_apply=%region_56.57 | all-reduce | flops 7488 | bytes 59904 | tf_op jit(solution)/shard_map/psum | solution.py:309
  902.0 8.0 all-reduce.1
  914.7 64.6 %reduce-scatter.35.cloned.1.call-done = f32[1536,48]{0,1:T(8,128)} async-done(((f32[1536,768]{0,1:T(8,128)}), f32[1536,48]{0,1:T(8,128)}) %reduce-scatter.35.cloned.1.call-update) | async-done | bytes 294928 | tf_op jit(solution)/shard_map/reduce_scatter | solution.py:295
  979.2 79.2 %reduce-scatter.33.cloned.1.call-done = f32[48,1536]{1,0:T(8,128)} async-done(((f32[768,1536]{1,0:T(8,128)}), f32[48,1536]{1,0:T(8,128)}) %reduce-scatter.33.cloned.1.call-update) | async-done | bytes 294928 | tf_op jit(solution)/shard_map/reduce_scatter | solution.py:294
  1058.5 71.9 %reduce-scatter.29.cloned.1.call-done = f32[48,3,384]{2,0,1:T(8,128)} async-done(((f32[768,3,384]{2,0,1:T(8,128)}), f32[48,3,384]{2,0,1:T(8,128)}) %reduce-scatter.29.cloned.1.call-update) | async-done | bytes 221200 | tf_op jit(solution)/shard_map/reduce_scatter | solution.py:292
  (521 shorter events, 284.4 us)
Async XLA Ops:
  7.2 47.5 %all-gather.18.cloned.1.call-start = ((), (), s32[]{:S(2)}) async-start(), calls=%async_computation.13 | async-start | bytes 1880064 | tf_op jit(solution)/shard_map/all_gather | solution.py:159
  8.0 75.4 %all-gather.16.cloned.1.call-start = ((), (), s32[]{:S(2)}) async-start(), calls=%async_computation.12 | async-start | bytes 2359296 | tf_op jit(solution)/shard_map/all_gather | solution.py:169
  12.2 100.5 %all-gather.26.cloned.1.call-start = ((), (), s32[]{:S(2)}) async-start(), calls=%async_computation.19 | async-start | bytes 2359296 | tf_op jit(solution)/shard_map/all_gather | solution.py:169
  12.3 14.1 %copy-start.100 = (bf16[384,48]{0,1:T(8,128)(2,1)S(1)}, bf16[384,48]{0,1:T(8,128)(2,1)}, u32[]{:S(2)}) copy-start(bf16[384,48]{0,1:T(8,128)(2,1)} %param.36) | copy-start | bytes 110596
  12.9 216.1 %reduce-scatter.17.cloned.1.call-start = ((), (), s32[]{:S(2)}) async-start(), calls=%async_computation.20 | async-start | bytes 2359296 | tf_op jit(solution)/shard_map/reduce_scatter | solution.py:192
  57.5 55.2 %copy-start.52 = (bf16[768,3,384]{0,2,1:T(8,128)(2,1)}, bf16[768,3,384]{0,2,1:T(8,128)(2,1)S(1)}, u32[]{:S(2)}) copy-start(bf16[768,3,384]{0,2,1:T(8,128)(2,1)S(1)} %copy.67) | copy-start | bytes 5308420
  134.0 16.7 %copy-start.55 = (f32[1024,6]{0,1:T(8,128)}, f32[1024,6]{0,1:T(8,128)S(1)}, u32[]{:S(2)}) copy-start(f32[1024,6]{0,1:T(8,128)S(1)} %broadcast_multiply_fusion.6) | copy-start | bytes 73732
  134.0 12.3 %copy-start.84 = (f32[2,512,6]{1,0,2:T(2,128)}, f32[2,512,6]{1,0,2:T(2,128)S(1)}, u32[]{:S(2)}) copy-start(f32[2,512,6]{1,0,2:T(2,128)S(1)} %div.111) | copy-start | bytes 73732
  136.4 14.3 %copy-start.68 = (f32[1024,6]{0,1:T(8,128)}, f32[1024,6]{0,1:T(8,128)S(1)}, u32[]{:S(2)}) copy-start(f32[1024,6]{0,1:T(8,128)S(1)} %add_rsqrt_fusion.2) | copy-start | bytes 73732
  136.5 14.2 %copy-start.57 = (f32[1024,6]{0,1:T(8,128)}, f32[1024,6]{0,1:T(8,128)S(1)}, u32[]{:S(2)}) copy-start(f32[1024,6]{0,1:T(8,128)S(1)} %broadcast_multiply_fusion.4) | copy-start | bytes 73732
  136.5 9.8 copy-start.86
  138.9 11.8 %copy-start.70 = (f32[1024,6]{0,1:T(8,128)}, f32[1024,6]{0,1:T(8,128)S(1)}, u32[]{:S(2)}) copy-start(f32[1024,6]{0,1:T(8,128)S(1)} %add_rsqrt_fusion) | copy-start | bytes 73732
  139.0 7.3 copy-start.87
  192.3 62.3 %reduce-scatter.13.cloned.1.call-start = ((), (), s32[]{:S(2)}) async-start(), calls=%async_computation.14 | async-start | bytes 2359296 | tf_op jit(solution)/shard_map/reduce_scatter | solution.py:192
  228.3 26.3 %copy-start.11 = (bf16[2,512,768]{2,1,0:T(8,128)(2,1)S(1)}, bf16[2,512,768]{2,1,0:T(8,128)(2,1)}, u32[]{:S(2)}) copy-start(bf16[2,512,768]{2,1,0:T(8,128)(2,1)} %param.26) | copy-start | bytes 4718596
  228.3 26.3 %copy-start.93 = (f32[768]{0:T(1024)S(1)}, f32[768]{0:T(1024)}, u32[]{:S(2)}) copy-start(f32[768]{0:T(1024)} %param.37) | copy-start | bytes 9220
  228.4 70.8 %all-gather.22.cloned.1.call-start = ((), (), s32[]{:S(2)}) async-start(), calls=%async_computation.16 | async-start | bytes 2506752 | tf_op jit(solution)/shard_map/all_gather | solution.py:161
  229.0 98.2 %all-gather.28.cloned.1.call-start = ((), (), s32[]{:S(2)}) async-start(), calls=%async_computation.21 | async-start | bytes 2359296 | tf_op jit(solution)/shard_map/all_gather | solution.py:201
  229.0 27.7 %copy-start.22 = (bf16[512,768]{1,0:T(8,128)(2,1)S(1)}, bf16[512,768]{1,0:T(8,128)(2,1)}, u32[]{:S(2)}) copy-start(bf16[512,768]{1,0:T(8,128)(2,1)} %reduce-scatter.17.cloned.1.call-done) | copy-start | bytes 2359300
  259.7 96.8 %all-gather.20.cloned.1.call-start = ((), (), s32[]{:S(2)}) async-start(), calls=%async_computation.15 | async-start | bytes 2359296 | tf_op jit(solution)/shard_map/all_gather | solution.py:201
  260.5 129.0 %all-gather.36.cloned.1.call-start = ((), (), s32[]{:S(2)}) async-start(), calls=%async_computation.34 | async-start | bytes 2359296 | tf_op jit(solution)/shard_map/all_gather | solution.py:222
  263.2 166.6 %all-gather.24.cloned.1.call-start = ((), (), s32[]{:S(2)}) async-start(), calls=%async_computation.17 | async-start | bytes 2506752 | tf_op jit(solution)/shard_map/all_gather | solution.py:162
  263.8 193.5 %all-gather.34.cloned.1.call-start = ((), (), s32[]{:S(2)}) async-start(), calls=%async_computation.33 | async-start | bytes 2359296 | tf_op jit(solution)/shard_map/all_gather | solution.py:222
  264.5 92.0 %copy-start.129 = (f32[1536]{0:T(1024)S(1)}, f32[1536]{0:T(1024)}, u32[]{:S(2)}) copy-start(f32[1536]{0:T(1024)} %param.41) | copy-start | bytes 18436
  264.5 222.2 %reduce-scatter.25.cloned.1.call-start = ((), (), s32[]{:S(2)}) async-start(), calls=%async_computation.26 | async-start | bytes 2359296 | tf_op jit(solution)/shard_map/reduce_scatter | solution.py:232
  429.8 12.6 %copy-start.124 = (bf16[768,1536]{1,0:T(8,128)(2,1)S(1)}, bf16[768,1536]{1,0:T(8,128)(2,1)}, u32[]{:S(2)}) copy-start(bf16[768,1536]{1,0:T(8,128)(2,1)} %all-gather.22.cloned.1.call-done) | copy-start | bytes 7077892
  446.2 68.4 %reduce-scatter.21.cloned.1.call-start = ((), (), s32[]{:S(2)}) async-start(), calls=%async_computation.23 | async-start | bytes 2359296 | tf_op jit(solution)/shard_map/reduce_scatter | solution.py:232
  457.3 12.6 %copy-start.125 = (bf16[768,1536]{1,0:T(8,128)(2,1)S(1)}, bf16[768,1536]{1,0:T(8,128)(2,1)}, u32[]{:S(2)}) copy-start(bf16[768,1536]{1,0:T(8,128)(2,1)} %all-gather.22.cloned.1.call-done) | copy-start | bytes 7077892
  473.6 69.2 %reduce-scatter.15.cloned.1.call-start = ((), (), s32[]{:S(2)}) async-start(), calls=%async_computation.18 | async-start | bytes 2359296 | tf_op jit(solution)/shard_map/reduce_scatter | solution.py:206
  480.1 91.0 %reduce-scatter.19.cloned.1.call-start = ((), (), s32[]{:S(2)}) async-start(), calls=%async_computation.22 | async-start | bytes 2359296 | tf_op jit(solution)/shard_map/reduce_scatter | solution.py:206
  486.6 84.5 %copy-start.120 = (f32[768]{0:T(1024)S(1)}, f32[768]{0:T(1024)}, u32[]{:S(2)}) copy-start(f32[768]{0:T(1024)} %param.43) | copy-start | bytes 9220
  486.6 122.5 %all-gather.32.cloned.1.call-start = ((), (), s32[]{:S(2)}) async-start(), calls=%async_computation.27 | async-start | bytes 2359296 | tf_op jit(solution)/shard_map/all_gather | solution.py:244
  581.8 97.4 %all-gather.30.cloned.1.call-start = ((), (), s32[]{:S(2)}) async-start(), calls=%async_computation.24 | async-start | bytes 2359296 | tf_op jit(solution)/shard_map/all_gather | solution.py:244
  582.5 26.6 %copy-start.67 = (bf16[384,768]{0,1:T(8,128)(2,1)S(1)}, bf16[384,768]{0,1:T(8,128)(2,1)}, u32[]{:S(2)}) copy-start(bf16[384,768]{0,1:T(8,128)(2,1)} %all_gather.57) | copy-start | bytes 1769476
  583.5 250.8 %reduce-scatter.27.cloned.1.call-start = ((), (), s32[]{:S(2)}) async-start(), calls=%async_computation.28 | async-start | bytes 2359296 | tf_op jit(solution)/shard_map/reduce_scatter | solution.py:278
  630.9 11.7 %copy-start.1 = (f32[6,512,1024]{2,1,0:T(8,128)S(1)}, f32[6,512,1024]{2,1,0:T(8,128)}, u32[]{:S(2)}) copy-start(f32[6,512,1024]{2,1,0:T(8,128)} %copy-done) | copy-start | bytes 37748740 | tf_op jit(solution)/shard_map/while/body/eval_jaxpr/while
  649.3 6.7 copy-start
  661.0 12.1 %copy-start.1 = (f32[6,512,1024]{2,1,0:T(8,128)S(1)}, f32[6,512,1024]{2,1,0:T(8,128)}, u32[]{:S(2)}) copy-start(f32[6,512,1024]{2,1,0:T(8,128)} %copy-done) | copy-start | bytes 37748740 | tf_op jit(solution)/shard_map/while/body/eval_jaxpr/while
  687.1 62.0 %copy-start.85 = (f32[2,512,6]{1,0,2:T(2,128)S(1)}, f32[2,512,6]{1,0,2:T(2,128)}, u32[]{:S(2)}) copy-start(f32[2,512,6]{1,0,2:T(2,128)} %copy-done.84) | copy-start | bytes 73732
  700.9 11.7 %copy-start.3 = (f32[6,512,1024]{2,1,0:T(8,128)S(1)}, f32[6,512,1024]{2,1,0:T(8,128)}, u32[]{:S(2)}) copy-start(f32[6,512,1024]{2,1,0:T(8,128)} %copy-done.2) | copy-start | bytes 37748740 | tf_op jit(solution)/shard_map/while/body/eval_jaxpr/while
  719.3 6.7 copy-start.2
  731.0 12.1 %copy-start.3 = (f32[6,512,1024]{2,1,0:T(8,128)S(1)}, f32[6,512,1024]{2,1,0:T(8,128)}, u32[]{:S(2)}) copy-start(f32[6,512,1024]{2,1,0:T(8,128)} %copy-done.2) | copy-start | bytes 37748740 | tf_op jit(solution)/shard_map/while/body/eval_jaxpr/while
  783.2 54.8 %reduce-scatter.23.cloned.1.call-start = ((), (), s32[]{:S(2)}) async-start(), calls=%async_computation.25 | async-start | bytes 2359296 | tf_op jit(solution)/shard_map/reduce_scatter | solution.py:278
  791.0 123.6 %reduce-scatter.31.cloned.1.call-start = ((), (), s32[]{:S(2)}) async-start(), calls=%async_computation.30 | async-start | bytes 1253376 | tf_op jit(solution)/shard_map/reduce_scatter | solution.py:293
  796.7 182.5 %reduce-scatter.35.cloned.1.call-start = ((), (), s32[]{:S(2)}) async-start(), calls=%async_computation.32 | async-start | bytes 5013504 | tf_op jit(solution)/shard_map/reduce_scatter | solution.py:295
  806.7 251.7 %reduce-scatter.33.cloned.1.call-start = ((), (), s32[]{:S(2)}) async-start(), calls=%async_computation.31 | async-start | bytes 5013504 | tf_op jit(solution)/shard_map/reduce_scatter | solution.py:294
  817.6 312.8 %reduce-scatter.29.cloned.1.call-start = ((), (), s32[]{:S(2)}) async-start(), calls=%async_computation.29 | async-start | bytes 3760128 | tf_op jit(solution)/shard_map/reduce_scatter | solution.py:292
  834.2 75.8 %copy-start.29 = (f32[512,768]{1,0:T(8,128)S(1)}, f32[512,768]{1,0:T(8,128)}, u32[]{:S(2)}) copy-start(f32[512,768]{1,0:T(8,128)} %get-tuple-element.656) | copy-start | bytes 4718596
  (119 other events, 368.3 us)
Sparse Core Ops, SparseCore 0:
  10.3 44.3 all-gather.17
  56.8 26.4 all-gather.15
  85.5 27.1 all-gather.25
  192.5 26.1 reduce-scatter.16
  228.5 26.1 reduce-scatter.12
  256.8 42.3 all-gather.21
  301.3 25.8 all-gather.27
  329.3 27.1 all-gather.19
  358.1 27.1 all-gather.35
  387.4 42.3 all-gather.23
  431.3 25.8 all-gather.33
  459.4 26.1 reduce-scatter.24
  488.4 26.1 reduce-scatter.20
  516.6 26.1 reduce-scatter.14
  544.9 26.1 reduce-scatter.18
  581.9 27.1 all-gather.31
  610.5 27.1 all-gather.29
  783.3 26.1 reduce-scatter.26
  811.8 26.1 reduce-scatter.22
  842.0 58.1 reduce-scatter.30
  904.6 74.5 reduce-scatter.34
  983.7 74.7 reduce-scatter.32
  1062.9 67.4 reduce-scatter.28
where the time goes:
time: 1140 us
  waiting for transfers between devices  541 us (47%)
  matrix products  283 us (25%)
  other arithmetic  111 us (10%)
  blocking collectives  105 us (9%)
  local copies, waits for them, and re-layouts  78.1 us (7%)
  between operations  15.9 us (1%)
    reduce_scatter x1, waiting for transfers between devices, on_device(): lax.psum_scatter(totals[2], 'fsdp', scatter_dimension=0, tiled=True)  79.2 us
    reduce_scatter x1, waiting for transfers between devices, on_device(): lax.psum_scatter(totals[0], 'fsdp', scatter_dimension=0, tiled=True)  71.9 us
    reduce_scatter x1, waiting for transfers between devices, on_device(): lax.psum_scatter(totals[3], 'fsdp', scatter_dimension=1, tiled=True)  64.6 us
    psum x1, blocking collectives, on_device(): lax.psum((grad_qkv_bias, grad_up_bias, grad_out_bias, grad_down_bias, gra...  61.2 us
    reduce_scatter x2, waiting for transfers between devices, on_device(): lax.psum_scatter(jnp.dot(down_piece, full_down, preferred_element_type=jn...  56.5 us
    all_gather x2, waiting for transfers between devices, on_device(): rows_two = lax.all_gather(normed2, 'tp', axis=0, tiled=True)  50 us
    all_gather x2, waiting for transfers between devices, on_device(): lax.all_gather(normed1, 'tp', axis=0, tiled=True)  43.2 us
    all_gather x1, waiting for transfers between devices, on_device(): lax.all_gather(down_weight, 'fsdp', axis=1, tiled=True)  40.3 us
  transfers between devices with their start and end apart: 23, of which 17 were waited for; matrix products, arithmetic and copies ran while one was open for 23% of the time, Pallas kernels for 0%

commit v1 on v0

v1 whole, which is shorter than its diff:
```python
from functools import partial

import jax
import jax.numpy as jnp
from jax import lax
from jax.experimental import pallas as pl
from jax.experimental.pallas import tpu as pltpu
from jax.sharding import PartitionSpec as P

LEN = 1024
IMG_MOST = 256
BLOCK = 256
REACH = -(-(IMG_MOST - 1) // BLOCK)
EPSILON = 1e-06
BF = jnp.bfloat16
F32 = jnp.float32


def norm_parts(values):
    average = jnp.mean(values, axis=-1, keepdims=True)
    centred = values - average
    spread = jnp.mean(centred * centred, axis=-1, keepdims=True)
    scaled = lax.rsqrt(spread + EPSILON)
    return (centred * scaled, scaled)


def norm_back(grad_out, unit, scaled, gain):
    grad_unit = grad_out * gain
    first = jnp.mean(grad_unit, axis=-1, keepdims=True)
    second = jnp.mean(grad_unit * unit, axis=-1, keepdims=True)
    return scaled * (grad_unit - first - unit * second)


def mm(a, b):
    return jnp.dot(a, b, preferred_element_type=F32)


def mm_nt(a, b):
    return lax.dot_general(a, b, (((1,), (1,)), ((), ())), preferred_element_type=F32)


def mm_tn(a, b):
    return lax.dot_general(a, b, (((0,), (0,)), ((), ())), preferred_element_type=F32)


def key_range(block, count):
    return max(0, block - REACH), min(count, block + REACH + 1)


def attend_kernel(
    x_ref, w_ref, b_ref, qg_ref, qb_ref, kg_ref, idc_ref, idr_ref, p_ref, mixed_ref, *, depth
):
    length = x_ref.shape[0]
    lanes = mixed_ref.shape[1]
    count = length // BLOCK
    scale = depth ** (-0.5)
    project = mm(x_ref[...], w_ref[0]) + b_ref[0]
    p_ref[0] = project
    heads = []
    for head in range(lanes // depth):
        part = [
            project[:, i * lanes + head * depth : i * lanes + (head + 1) * depth] for i in range(3)
        ]
        query = (norm_parts(part[0])[0] * qg_ref[...] + qb_ref[...]).astype(BF)
        query = query * jnp.asarray(scale, BF)
        key = (norm_parts(part[1])[0] * kg_ref[...]).astype(BF)
        value = part[2].astype(BF)
        value = jnp.concatenate([value, jnp.ones_like(value)], axis=1)
        rows = []
        for block in range(count):
            low, high = key_range(block, count)
            q = slice(block * BLOCK, (block + 1) * BLOCK)
            k = slice(low * BLOCK, high * BLOCK)
            scores = mm_nt(query[q], key[k])
            same = idc_ref[q, :] == idr_ref[:, k]
            weights = jnp.where(same, jnp.exp(scores), 0.0).astype(BF)
            both = mm(weights, value[k])
            rows.append(both[:, :depth] / both[:, depth : depth + 1])
        heads.append(jnp.concatenate(rows, axis=0))
    mixed_ref[...] = jnp.concatenate(heads, axis=1).astype(BF)


def attend_back_kernel(
    g_ref, w_ref, p_ref, qg_ref, qb_ref, kg_ref, idc_ref, idr_ref, gp_ref, sums_ref, *, depth
):
    length = g_ref.shape[0]
    lanes = w_ref.shape[2]
    count = length // BLOCK
    scale = depth ** (-0.5)
    grad_mixed = mm(g_ref[...], w_ref[0]).astype(BF)
    project = p_ref[0]
    sums = [jnp.zeros((1, depth), F32) for _ in range(3)]
    columns = [[], [], []]
    for head in range(lanes // depth):
        part = [
            project[:, i * lanes + head * depth : i * lanes + (head + 1) * depth] for i in range(3)
        ]
        query_unit, query_scaled = norm_parts(part[0])
        key_unit, key_scaled = norm_parts(part[1])
        query = (query_unit * qg_ref[...] + qb_ref[...]).astype(BF)
        query = query * jnp.asarray(scale, BF)
        key = (key_unit * kg_ref[...]).astype(BF)
        value = part[2].astype(BF)
        grad = grad_mixed[:, head * depth : (head + 1) * depth]
        grad_key = [None] * count
        grad_value = [None] * count
        grad_query = []
        for block in range(count):
            low, high = key_range(block, count)
            q = slice(block * BLOCK, (block + 1) * BLOCK)
            k = slice(low * BLOCK, high * BLOCK)
            scores = mm_nt(key[k], query[q])
            same = idc_ref[k, :] == idr_ref[:, q]
            raised = jnp.where(same, jnp.exp(scores), 0.0)
            weights = raised * (1.0 / jnp.sum(raised, axis=0, keepdims=True))
            grad_weights = mm_nt(value[k], grad[q])
            inner = jnp.sum(grad_weights * weights, axis=0, keepdims=True)
            grad_scores = (weights * (grad_weights - inner)).astype(BF)
            grad_query.append(mm_tn(grad_scores, key[k]) * scale)
            to_key = mm(grad_scores, query[q])
            to_value = mm(weights.astype(BF), grad[q])
            for i in range(low, high):
                piece = slice((i - low) * BLOCK, (i - low + 1) * BLOCK)
                grad_key[i] = to_key[piece] if grad_key[i] is None else grad_key[i] + to_key[piece]
                grad_value[i] = (
                    to_value[piece] if grad_value[i] is None else grad_value[i] + to_value[piece]
                )
        grad_query = jnp.concatenate(grad_query, axis=0)
        grad_key = jnp.concatenate(grad_key, axis=0)
        grad_value = jnp.concatenate(grad_value, axis=0)
        sums[0] += jnp.sum(grad_query * query_unit, axis=0, keepdims=True)
        sums[1] += jnp.sum(grad_query, axis=0, keepdims=True)
        sums[2] += jnp.sum(grad_key * key_unit, axis=0, keepdims=True)
        columns[0].append(norm_back(grad_query, query_unit, query_scaled, qg_ref[...]))
        columns[1].append(norm_back(grad_key, key_unit, key_scaled, kg_ref[...]))
        columns[2].append(grad_value)
    for i in range(3):
        gp_ref[0, :, i * lanes : (i + 1) * lanes] = jnp.concatenate(columns[i], axis=1).astype(BF)

    @pl.when(pl.program_id(0) == 0)
    def _():
        sums_ref[...] = jnp.zeros_like(sums_ref)

    for i in range(3):
        sums_ref[i : i + 1, :] += sums[i]


def attend(normed, weight, bias, query_gain, query_bias, key_gain, ids, local_width):
    length, width = normed.shape
    tp = weight.shape[0]
    depth = query_gain.shape[0]
    lanes = 2 * depth
    per = local_width // lanes
    whole = lambda *shape: pl.BlockSpec(shape, lambda i: (0,) * len(shape))
    return pl.pallas_call(
        partial(attend_kernel, depth=depth),
        grid=(tp * per,),
        in_specs=[
            whole(length, width),
            pl.BlockSpec((1, width, 3 * lanes), lambda i: (i // per, 0, i % per)),
            pl.BlockSpec((1, 1, 3 * lanes), lambda i: (i // per, 0, i % per)),
            whole(1, depth),
            whole(1, depth),
            whole(1, depth),
            whole(length, 1),
            whole(1, length),
        ],
        out_specs=[
            pl.BlockSpec((1, length, 3 * lanes), lambda i: (i // per, 0, i % per)),
            pl.BlockSpec((length, lanes), lambda i: (0, i)),
        ],
        out_shape=[
            jax.ShapeDtypeStruct((tp, length, 3 * local_width), F32),
            jax.ShapeDtypeStruct((length, tp * local_width), BF),
        ],
        compiler_params=pltpu.CompilerParams(vmem_limit_bytes=56 * 2**20),
        cost_estimate=pl.CostEstimate(
            flops=2 * length * width * 3 * local_width * tp,
            bytes_accessed=length * local_width * tp * 16,
            transcendentals=length * 3 * BLOCK * tp * local_width // depth,
        ),
        name="attend",
    )(
        normed,
        weight,
        bias,
        query_gain[None],
        query_bias[None],
        key_gain[None],
        ids[:, None],
        ids[None],
    )


def attend_back(
    grad_rows, weight, out_column, project, query_gain, query_bias, key_gain, ids, local_width
):
    length, width = grad_rows.shape
    tp = weight.shape[0]
    depth = query_gain.shape[0]
    lanes = 2 * depth
    per = local_width // lanes
    first = out_column // lanes
    whole = lambda *shape: pl.BlockSpec(shape, lambda i: (0,) * len(shape))
    return pl.pallas_call(
        partial(attend_back_kernel, depth=depth),
        grid=(tp * per,),
        in_specs=[
            whole(length, width),
            pl.BlockSpec((1, width, lanes), lambda i: (i // per, 0, first + i % per)),
            pl.BlockSpec((1, length, 3 * lanes), lambda i: (i // per, 0, i % per)),
            whole(1, depth),
            whole(1, depth),
            whole(1, depth),
            whole(length, 1),
            whole(1, length),
        ],
        out_specs=[
            pl.BlockSpec((1, length, 3 * lanes), lambda i: (i // per, 0, i % per)),
            whole(3, depth),
        ],
        out_shape=[
            jax.ShapeDtypeStruct((tp, length, 3 * local_width), BF),
            jax.ShapeDtypeStruct((3, depth), F32),
        ],
        compiler_params=pltpu.CompilerParams(vmem_limit_bytes=56 * 2**20),
        cost_estimate=pl.CostEstimate(
            flops=8 * length * width * local_width * tp,
            bytes_accessed=length * local_width * tp * 18,
            transcendentals=length * 3 * BLOCK * tp * local_width // depth,
        ),
        name="attend_back",
    )(
        grad_rows,
        weight,
        project,
        query_gain[None],
        query_bias[None],
        key_gain[None],
        ids[:, None],
        ids[None],
    )


def on_device(
    inputs,
    image_ids,
    cotangent,
    norm1_gain,
    norm1_bias,
    qkv_weight,
    qkv_bias,
    query_gain,
    query_bias,
    key_gain,
    out_weight,
    out_bias,
    norm2_gain,
    norm2_bias,
    up_weight,
    up_bias,
    down_weight,
    down_bias,
):
    batches, rows_here, width = inputs.shape
    tp = lax.axis_size("tp")
    me = lax.axis_index("tp")
    assert batches == 2 and tp == 2 and rows_here * tp == LEN
    everyone = ("tp", "fsdp")
    shard = qkv_weight.shape[0]
    local_width = qkv_weight.shape[2]
    local_hidden = up_weight.shape[1]
    lanes = 2 * query_gain.shape[0]
    per = local_width // lanes
    swap = [(0, 1), (1, 0)]

    def pick(array, index):
        return lax.dynamic_index_in_dim(array, index, 0, keepdims=False)

    def in_order(own, other):
        return jnp.where(
            me == 0, jnp.concatenate([own, other], 0), jnp.concatenate([other, own], 0)
        )

    def to_sequence(array):
        return in_order(pick(array, me), lax.ppermute(pick(array, 1 - me), "tp", swap))

    def from_sequence(array, dtype):
        halves = array.reshape(2, rows_here, width)
        other = lax.ppermute(pick(halves, 1 - me).astype(dtype), "tp", swap).astype(array.dtype)
        own = pick(halves, me)
        return jnp.where(me == 0, jnp.stack([own, other]), jnp.stack([other, own]))

    packed = jnp.concatenate(
        [
            qkv_weight.reshape(shard, 3, per, lanes).transpose(0, 2, 1, 3).reshape(shard, -1),
            out_weight.T,
            up_weight,
            down_weight.T,
        ],
        axis=1,
    )
    gathered = lax.all_gather(packed, everyone, axis=0, tiled=True).reshape(tp, width, -1)
    edge_out = 3 * local_width
    edge_up = edge_out + local_width
    edge_down = edge_up + local_hidden
    out_t = [gathered[i, :, edge_out:edge_up] for i in range(tp)]
    up = [gathered[i, :, edge_up:edge_down] for i in range(tp)]
    down_t = [gathered[i, :, edge_down:] for i in range(tp)]
    qkv = [gathered[i, :, :edge_out] for i in range(tp)]

    biases = jnp.concatenate(
        [qkv_bias.reshape(3, per, lanes).transpose(1, 0, 2).reshape(-1), up_bias]
    )
    biases = in_order(biases[None], lax.ppermute(biases, "tp", swap)[None])
    qkv_bias_all = biases[:, None, :edge_out]
    up_bias_all = biases[:, edge_out:]

    tokens_in = to_sequence(inputs).astype(F32)
    ids = to_sequence(image_ids)
    grad_low = to_sequence(cotangent)
    grad_y = grad_low.astype(F32)

    unit_one, scaled_one = norm_parts(tokens_in)
    normed1 = (unit_one * norm1_gain + norm1_bias).astype(BF)
    project, mixed = attend(
        normed1, gathered, qkv_bias_all, query_gain, query_bias, key_gain, ids, local_width
    )
    resid = tokens_in + out_bias
    for i in range(tp):
        resid = resid + mm_nt(mixed[:, i * local_width : (i + 1) * local_width], out_t[i])
    unit_two, scaled_two = norm_parts(resid)
    normed2 = (unit_two * norm2_gain + norm2_bias).astype(BF)

    output = resid + down_bias
    hidden, slope = [], []
    for i in range(tp):
        preact = mm(normed2, up[i]) + up_bias_all[i]
        half = 0.5 * (1.0 + lax.erf(preact * (0.5**0.5)))
        bell = jnp.exp(-0.5 * preact * preact) * ((0.5 / jnp.pi) ** 0.5)
        hidden.append((preact * half).astype(BF))
        slope.append((half + preact * bell).astype(BF))
        output = output + mm_nt(hidden[i], down_t[i])
    output = from_sequence(output.astype(BF), BF)

    grad_normed2 = 0.0
    terms_up, terms_down, sums_up = [], [], []
    for i in range(tp):
        grad_preact = (mm(grad_low, down_t[i]) * slope[i].astype(F32)).astype(BF)
        grad_normed2 = grad_normed2 + mm_nt(grad_preact, up[i])
        terms_up.append(mm_tn(normed2, grad_preact).astype(BF))
        terms_down.append(mm_tn(grad_low, hidden[i]).astype(BF))
        sums_up.append(jnp.sum(grad_preact.astype(F32), axis=0))
    late = jnp.stack(
        [jnp.concatenate([terms_up[i], terms_down[i]], axis=1) for i in range(tp)]
    ).reshape(tp * width, -1)
    late = lax.psum_scatter(late, everyone, scatter_dimension=0, tiled=True).astype(F32)
    up_weight_grad = late[:, :local_hidden]
    down_weight_grad = late[:, local_hidden:].T

    grad_resid = grad_y + norm_back(grad_normed2, unit_two, scaled_two, norm2_gain)
    grad_resr = grad_resid.astype(BF)
    grad_project, head_sums = attend_back(
        grad_resr,
        gathered,
        edge_out,
        project,
        query_gain,
        query_bias,
        key_gain,
        ids,
        local_width,
    )
    grad_normed1 = 0.0
    terms_qkv, terms_out, sums_qkv = [], [], []
    for i in range(tp):
        grad_normed1 = grad_normed1 + mm_nt(grad_project[i], qkv[i])
        terms_qkv.append(mm_tn(normed1, grad_project[i]).astype(BF))
        terms_out.append(
            mm_tn(grad_resr, mixed[:, i * local_width : (i + 1) * local_width]).astype(BF)
        )
        sums_qkv.append(jnp.sum(grad_project[i].astype(F32), axis=0))
    early = jnp.stack(
        [jnp.concatenate([terms_qkv[i], terms_out[i]], axis=1) for i in range(tp)]
    ).reshape(tp * width, -1)
    early = lax.psum_scatter(early, everyone, scatter_dimension=0, tiled=True).astype(F32)
    qkv_weight_grad = (
        early[:, :edge_out]
        .reshape(shard, per, 3, lanes)
        .transpose(0, 2, 1, 3)
        .reshape(qkv_weight.shape)
    )
    out_weight_grad = early[:, edge_out:].T

    input_grad = grad_resid + norm_back(grad_normed1, unit_one, scaled_one, norm1_gain)
    input_grad = from_sequence(input_grad, BF)

    vectors = [
        jnp.sum(grad_normed1 * unit_one, axis=0),
        jnp.sum(grad_normed1, axis=0),
        head_sums[0],
        head_sums[1],
        head_sums[2],
        jnp.sum(grad_resid, axis=0),
        jnp.sum(grad_normed2 * unit_two, axis=0),
        jnp.sum(grad_normed2, axis=0),
        jnp.sum(grad_y, axis=0),
        *sums_qkv,
        *sums_up,
    ]
    summed = lax.psum(jnp.concatenate(vectors), everyone)
    pieces, start = [], 0
    for vector in vectors:
        pieces.append(summed[start : start + vector.shape[0]])
        start += vector.shape[0]
    gain_one, shift_one, gain_query, shift_query, gain_key = pieces[:5]
    sum_out, gain_two, shift_two, sum_down = pieces[5:9]
    qkv_bias_grad = jnp.where(me == 0, pieces[9], pieces[10])
    qkv_bias_grad = qkv_bias_grad.reshape(per, 3, lanes).transpose(1, 0, 2).reshape(qkv_bias.shape)
    up_bias_grad = jnp.where(me == 0, pieces[11], pieces[12])
    return (
        output,
        input_grad,
        gain_one,
        shift_one,
        qkv_weight_grad,
        qkv_bias_grad,
        gain_query,
        shift_query,
        gain_key,
        out_weight_grad,
        sum_out,
        gain_two,
        shift_two,
        up_weight_grad,
        up_bias_grad,
        down_weight_grad,
        sum_down,
    )


def solution(mesh):
    placed = (
        P(None, ("fsdp", "tp"), None),
        P(None, ("fsdp", "tp")),
        P(None, ("fsdp", "tp"), None),
        P(),
        P(),
        P("fsdp", None, "tp"),
        P(None, "tp"),
        P(),
        P(),
        P(),
        P("tp", "fsdp"),
        P(),
        P(),
        P(),
        P("fsdp", "tp"),
        P("tp"),
        P("tp", "fsdp"),
        P(),
    )
    return jax.shard_map(
        on_device,
        mesh=mesh,
        in_specs=placed,
        out_specs=(
            P(None, ("fsdp", "tp"), None),
            P(None, ("fsdp", "tp"), None),
            P(),
            P(),
            P("fsdp", None, "tp"),
            P(None, "tp"),
            P(),
            P(),
            P(),
            P("tp", "fsdp"),
            P(),
            P(),
            P(),
            P("fsdp", "tp"),
            P("tp"),
            P("tp", "fsdp"),
            P(),
        ),
        check_vma=False,
    )
```

time: 1140 us -> 565 us (0.50)
  waiting for transfers between devices: 541 us -> 226 us
  matrix products: 283 us -> 79.8 us
  Pallas kernels: 0 us -> 111 us
  other arithmetic: 111 us -> 40.4 us
  local copies, waits for them, and re-layouts: 78.1 us -> 18 us
  blocking collectives: 105 us -> 65 us
    reduce_scatter x12 -> x2, waiting for transfers between devices: 329 us -> 123 us  [the longest x1 123 us: on_device(): lax.psum_scatter(late, everyone, scatter_dimension=0, tiled=True)]
    dot_general x52 -> x20, matrix products: 283 us -> 79.8 us  [the longest x8 29.6 us: mm_nt(): lax.dot_general(a, b, (((1,), (1,)), ((), ())), preferred_element_type=F32)]
    all_gather x11 -> x1, waiting for transfers between devices: 207 us -> 84.9 us  [on_device(): lax.all_gather(packed, everyone, axis=0, tiled=True).reshape(tp, width, -1)]
    pallas_call x0 -> x2, Pallas kernels: none -> 111 us  [the longest x1 69.2 us: attend_back(): pl.pallas_call(partial(attend_back_kernel, depth=depth), grid=(tp * per,)...]
    reduce_sum x14 -> x2, other arithmetic: 46.5 us -> 4.6 us  [the longest x1 3.88 us: on_device(): jnp.sum(grad_resid, axis=0)]
    all_gather x3 -> x0, blocking collectives: 35.4 us -> none  [the longest x1 25.8 us: on_device(): lax.all_gather(out_weight, 'fsdp', axis=1, tiled=True)]
    convert_element_type x10 -> x5, other arithmetic: 32.7 us -> 5.72 us  [the longest x1 3.08 us: on_device(): normed1 = (unit_one * norm1_gain + norm1_bias).astype(BF)]
    unnamed x253 -> x71, local copies, waits for them, and re-layouts: 26.1 us -> 2.71 us
  transfers between devices with their start and end apart: 23 -> 9, of which waited for: 17 -> 3; matrix products, arithmetic and copies ran while one was open for 23% -> 17% of each run, Pallas kernels for 0% -> 7%
where the time goes in v1:
time: 565 us; the launch traced here: 562 us
  waiting for transfers between devices  226 us (40%)
  Pallas kernels  111 us (20%)
  matrix products  79.8 us (14%)
  blocking collectives  65 us (12%)
  other arithmetic  40.4 us (7%)
  local copies, waits for them, and re-layouts  18 us (3%)
  between operations  14.8 us (3%)
  starting transfers between devices  7.26 us (1%)
    reduce_scatter x1, waiting for transfers between devices, on_device(): lax.psum_scatter(late, everyone, scatter_dimension=0, tiled=True)  123 us
    all_gather x1, waiting for transfers between devices, on_device(): lax.all_gather(packed, everyone, axis=0, tiled=True).reshape(tp, width, -1)  84.9 us
    pallas_call x1, Pallas kernels, attend_back(): pl.pallas_call(partial(attend_back_kernel, depth=depth), grid=(tp * per,)...  69.2 us
    psum x1, blocking collectives, on_device(): summed = lax.psum(jnp.concatenate(vectors), everyone)  65 us
    pallas_call x1, Pallas kernels, attend(): pl.pallas_call(partial(attend_kernel, depth=depth), grid=(tp * per,), in_...  41.9 us
    dot_general x8, matrix products, mm_nt(): lax.dot_general(a, b, (((1,), (1,)), ((), ())), preferred_element_type=F32)  29.6 us
    dot_general x4, matrix products, mm(): return jnp.dot(a, b, preferred_element_type=F32)  25.6 us
    dot_general x8, matrix products, mm_tn(): lax.dot_general(a, b, (((0,), (0,)), ((), ())), preferred_element_type=F32)  24.6 us
  transfers between devices with their start and end apart: 9, of which 3 were waited for; matrix products, arithmetic and copies ran while one was open for 17% of the time, Pallas kernels for 7%

profile of v1, /device:TPU:0, one launch (start us, length us, event | category | flops | bytes accessed | tf_op | source)
XLA Modules:
  0.0 561.9 jit_solution(2423772351686490083)
XLA Ops:
  7.2 1.0 reshape.230
  8.5 1.8 pad_maximum_fusion.2
  11.1 3.0 collective-permute-start.2
  15.8 2.1 collective-permute-start
  17.9 1.4 dynamic-slice_bitcast_fusion.1
  21.9 17.5 %collective-permute-done = bf16[512,768]{1,0:T(8,128)(2,1)S(1)} collective-permute-done((bf16[512,768]{1,0:T(8,128)(2,1)S(1)}, bf16[512,768]{1,0:T(8,128)(2,1)S(1)}, u32[]{:S(2)}, u32[]{:S(2)}) %collective-permute-start) | collective-permute-done | bytes 786464 | tf_op jit(solution)/shard_map/ppermute | solution.py:286
  40.8 3.1 fusion.17.x_ref
  43.8 84.9 %all-gather.2.cloned.1.call-done = bf16[1536,4608]{1,0:T(8,128)(2,1)} async-done(((bf16[48,4608]{1,0:T(8,128)(2,1)}), bf16[1536,4608]{1,0:T(8,128)(2,1)}) %all-gather.2.cloned.1.call-update) | async-done | bytes 14155792 | tf_op jit(solution)/shard_map/all_gather | solution.py:303
  128.8 41.9 %attend.1 = (f32[2,1024,1152]{2,1,0:T(8,128)}, bf16[1024,768]{1,0:T(8,128)(2,1)}) custom-call(bf16[1024,768]{1,0:T(8,128)(2,1)} %fusion.17.x_ref, bf16[2,768,4608]{2,1,0:T(8,128)(2,1)} %bitcast.142, f32[2,1,1152]{2,1,0:T(1,128)} %broadcast_in_dim.14.b_ref, f32[1,64]{1,0:T(1,128)} %bitcast.171, f32[1,64]{1,0:T(1,128)} %bitcast.173, f32[1,64]{1,0:T(1,128)} %bitcast.175, ...), custom_call_target="tpu_custom_call" | custom-call | flops 3623878656 | bytes 12582912 | tf_op jit(solution)/shard_map/attend/pallas_call | solution.py:155
  170.7 2.5 fusion.50
  173.2 2.5 fusion.55
  176.3 0.9 copy-done.21
  178.5 5.7 %multiply_convert_fusion.2 = (bf16[1024,1536]{1,0:T(8,128)(2,1)}, f32[1024,1536]{1,0:T(8,128)}) fusion(f32[1536]{0:T(1024)S(1)} %get-tuple-element.35, bf16[1024,768]{1,0:T(8,128)(2,1)S(1)} %add_convert_fusion.1, bf16[2,768,4608]{2,1,0:T(8,128)(2,1)S(1)} %bitcast.150), kind=kOutput, calls=%fused_computation.17 | convolution fusion | flops 2425356288 | bytes 13377536 | tf_op jit(solution)/shard_map/dot_general | solution.py:35
  184.2 5.1 multiply_convert_fusion.3
  189.3 7.0 %convert_reduce_fusion.1 = (f32[1536]{0:T(1024)S(1)}, bf16[1024,1536]{1,0:T(8,128)(2,1)S(1)}) fusion(f32[1024,1536]{1,0:T(8,128)S(1)} %get-tuple-element.65, f32[1536]{0:T(1024)S(1)} %get-tuple-element.36, bf16[2,768,4608]{2,1,0:T(8,128)(2,1)S(1)} %bitcast.152, bf16[512,768]{1,0:T(8,128)(2,1)} %collective-permute-done.4, ...), kind=kOutput, calls=%fused_computation.14 | convolution fusion | flops 2446588416 | bytes 13383681 | tf_op jit(solution)/shard_map/dot_general | solution.py:35
  196.3 2.6 fusion.32
  199.0 7.8 %convert_reduce_fusion = (f32[1536]{0:T(1024)S(1)}, bf16[1024,1536]{1,0:T(8,128)(2,1)S(1)}) fusion(f32[1024,1536]{1,0:T(8,128)} %get-tuple-element.67, f32[1536]{0:T(1024)S(1)} %get-tuple-element.35, bf16[2,768,4608]{2,1,0:T(8,128)(2,1)S(1)} %bitcast.154, bf16[512,768]{1,0:T(8,128)(2,1)} %collective-permute-done.4, bf16[512,768]{1,0:T(8,128)(2,1)S(1)} %copy-done.11, ...), kind=kOutput, calls=%fused_computation.13 | convolution fusion | flops 2446588416 | bytes 13383681 | tf_op jit(solution)/shard_map/dot_general | solution.py:35
  206.8 3.5 multiply_reduce_fusion
  210.3 3.9 fusion.52
  214.3 1.0 convolution_convert_fusion.6
  216.3 1.0 convolution_convert_fusion.7
  217.3 69.2 %attend_back.1 = (bf16[2,1024,1152]{2,1,0:T(8,128)(2,1)}, f32[3,64]{1,0:T(4,128)}) custom-call(bf16[1024,768]{1,0:T(8,128)(2,1)} %copy-done.9, bf16[2,768,4608]{2,1,0:T(8,128)(2,1)} %bitcast.145, f32[2,1024,1152]{2,1,0:T(8,128)} %get-tuple-element.22.p_ref, f32[1,64]{1,0:T(1,128)} %bitcast.172, f32[1,64]{1,0:T(1,128)} %bitcast.174, f32[1,64]{1,0:T(1,128)} %bitcast.176, ...), custom_call_target="tpu_custom_call" | custom-call | flops 4831838208 | bytes 14155776 | tf_op jit(solution)/shard_map/attend_back/pallas_call | solution.py:205
  286.5 4.1 convolution_convert_fusion.5
  290.6 2.3 convolution_convert_fusion.4
  293.3 2.5 pad_maximum_fusion.1
  295.9 5.6 %convolution_convert_fusion = bf16[768,1536]{1,0:T(8,128)(2,1)S(1)} fusion(bf16[1024,1536]{1,0:T(8,128)(2,1)} %get-tuple-element.66, bf16[512,768]{1,0:T(8,128)(2,1)} %collective-permute-done.4, bf16[512,768]{1,0:T(8,128)(2,1)} %get-tuple-element.40, pred[]{:T(512)S(6)} %eq.2), kind=kOutput, calls=%fused_computation.37 | convolution fusion | flops 2424176640 | bytes 7077889 | tf_op jit(solution)/shard_map/dot_general | solution.py:43
  301.6 4.7 convolution_convert_fusion.2
  306.3 2.9 convolution_convert_fusion.1
  309.3 2.9 convolution_convert_fusion.3
  312.2 4.3 maximum_bitcast_fusion
  316.6 8.4 %pad_maximum_fusion = bf16[2,768,3072]{2,1,0:T(8,128)(2,1)} fusion(bf16[1,768,3072]{2,1,0:T(8,128)(2,1)} %get-tuple-element.77, bf16[1,768,3072]{2,1,0:T(8,128)(2,1)} %get-tuple-element.76), kind=kLoop, calls=%fused_computation.2 | loop fusion | flops 4718592 | bytes 18874368 | tf_op jit(solution)/shard_map/stack | solution.py:354
  325.0 5.5 fusion.34
  330.6 4.5 add_convert_fusion
  335.1 1.2 constant_dynamic-slice_fusion.1
  336.3 1.4 collective-permute-start.3
  337.8 3.7 fusion.27
  341.5 4.8 fusion.22
  346.4 2.7 fusion.21
  349.1 1.0 fusion.46
  351.5 65.0 %psum.7 = f32[10176]{0:T(1024)S(1)} all-reduce(f32[10176]{0:T(1024)S(1)} %concatenate.98), channel_id=1, replica_groups=mesh['fsdp'=16,'tp'=2] {'tp','fsdp'}, use_global_device_ids=true, to_apply=%region_18.19 | all-reduce | flops 10176 | bytes 81408 | tf_op jit(solution)/shard_map/psum | solution.py:411
  419.2 2.8 maximum_select_fusion.2
  422.0 1.3 bitcast_convert_fusion
  423.3 1.9 maximum_select_fusion
  425.2 0.9 slice.162
  427.1 0.9 convert_element_type.115
  428.7 123.1 %reduce-scatter.5.cloned.1.call-done = bf16[48,3072]{1,0:T(8,128)(2,1)} async-done(((bf16[1536,3072]{1,0:T(8,128)(2,1)}), bf16[48,3072]{1,0:T(8,128)(2,1)}) %reduce-scatter.5.cloned.1.call-update) | async-done | bytes 294928 | tf_op jit(solution)/shard_map/reduce_scatter | solution.py:357
  551.7 1.0 convert_element_type.120
  553.5 1.6 slice.172
  (132 shorter events, 16.5 us)
Async XLA Ops:
  7.2 8.5 %copy-start.14 = (bf16[2,512,768]{2,1,0:T(8,128)(2,1)S(1)}, bf16[2,512,768]{2,1,0:T(8,128)(2,1)}, u32[]{:S(2)}) copy-start(bf16[2,512,768]{2,1,0:T(8,128)(2,1)} %param.18) | copy-start | bytes 4718596
  7.2 121.6 %all-gather.2.cloned.1.call-start = ((), (), s32[]{:S(2)}) async-start(), calls=%async_computation.2 | async-start | bytes 14598144 | tf_op jit(solution)/shard_map/all_gather | solution.py:303
  10.3 414.9 %reduce-scatter.3.cloned.1.call-start = ((), (), s32[]{:S(2)}) async-start(), calls=%async_computation.3 | async-start | bytes 4866048 | tf_op jit(solution)/shard_map/reduce_scatter | solution.py:386
  11.1 8.1 %collective-permute-start.2 = (s32[512]{0:T(512)S(1)}, s32[512]{0:T(512)S(1)}, u32[]{:S(2)}, u32[]{:S(2)}) collective-permute-start(s32[512]{0:T(512)S(1)} %bitcast.170), channel_id=1, source_target_pairs={{0,1},{1,0},{2,3},{3,2},{4,5},{5,4},{6,7},{7,6},{8,9},{9,8},{10,11... | collective-permute-start | bytes 6152 | tf_op jit(solution)/shard_map/ppermute | solution.py:286
  14.8 3.0 copy-start.15
  15.6 5.6 collective-permute-start.1
  15.8 25.0 %copy-start.2 = (bf16[512,768]{1,0:T(8,128)(2,1)}, bf16[512,768]{1,0:T(8,128)(2,1)S(1)}, u32[]{:S(2)}) copy-start(bf16[512,768]{1,0:T(8,128)(2,1)S(1)} %get-tuple-element.45) | copy-start | bytes 2359300
  15.8 23.7 %collective-permute-start = (bf16[512,768]{1,0:T(8,128)(2,1)S(1)}, bf16[512,768]{1,0:T(8,128)(2,1)S(1)}, u32[]{:S(2)}, u32[]{:S(2)}) collective-permute-start(bf16[512,768]{1,0:T(8,128)(2,1)S(1)} %get-tuple-element.44), channel_id=1, source_target_pairs={{0,1},{1,0},{2,3},{3,2},{4,5},{5,4},{6,7},{7,6},{8,9},{9,8},{10,11... | collective-permute-start | bytes 2359304 | tf_op jit(solution)/shard_map/ppermute | solution.py:286
  19.2 21.5 %copy-start.20 = (f32[768]{0:T(1024)S(1)}, f32[768]{0:T(1024)}, u32[]{:S(2)}) copy-start(f32[768]{0:T(1024)} %param.21) | copy-start | bytes 9220
  19.2 21.5 %copy-start.22 = (f32[768]{0:T(1024)S(1)}, f32[768]{0:T(1024)}, u32[]{:S(2)}) copy-start(f32[768]{0:T(1024)} %param.22) | copy-start | bytes 9220
  19.2 170.1 %collective-permute-start.4 = (bf16[512,768]{1,0:T(8,128)(2,1)}, bf16[512,768]{1,0:T(8,128)(2,1)}, u32[]{:S(2)}, u32[]{:S(2)}) collective-permute-start(bf16[512,768]{1,0:T(8,128)(2,1)} %get-tuple-element.41), channel_id=1, source_target_pairs={{0,1},{1,0},{2,3},{3,2},{4,5},{5,4},{6,7},{7,6},{8,9},{9,8},{10,11... | collective-permute-start | bytes 2359304 | tf_op jit(solution)/shard_map/ppermute | solution.py:286
  39.5 4.4 copy-start.6
  170.7 2.5 copy-start.3
  170.7 2.5 copy-start.7
  170.7 2.5 copy-start.19
  170.7 2.5 copy-start.25
  173.2 5.2 copy-start.5
  175.8 1.4 copy-start.21
  175.8 1.5 copy-start.23
  177.8 6.4 %copy-start.16 = (bf16[1024,768]{1,0:T(8,128)(2,1)}, bf16[1024,768]{1,0:T(8,128)(2,1)S(1)}, u32[]{:S(2)}) copy-start(bf16[1024,768]{1,0:T(8,128)(2,1)S(1)} %add_convert_fusion.1) | copy-start | bytes 4718596
  184.2 5.2 copy-start.11
  196.3 2.6 copy-start.27
  206.8 3.5 copy-start.29
  214.2 1.7 copy-start
  214.3 2.0 copy-start.9
  217.3 69.2 %copy-start.18 = (bf16[1024,768]{1,0:T(8,128)(2,1)S(1)}, bf16[1024,768]{1,0:T(8,128)(2,1)}, u32[]{:S(2)}) copy-start(bf16[1024,768]{1,0:T(8,128)(2,1)} %fusion.17.x_ref) | copy-start | bytes 4718596
  286.5 4.1 copy-start.10
  295.8 255.9 %reduce-scatter.5.cloned.1.call-start = ((), (), s32[]{:S(2)}) async-start(), calls=%async_computation.4 | async-start | bytes 9732096 | tf_op jit(solution)/shard_map/reduce_scatter | solution.py:357
  295.8 5.7 %copy-start.12 = (bf16[512,768]{1,0:T(8,128)(2,1)S(1)}, bf16[512,768]{1,0:T(8,128)(2,1)}, u32[]{:S(2)}) copy-start(bf16[512,768]{1,0:T(8,128)(2,1)} %get-tuple-element.40) | copy-start | bytes 2359300
  295.9 5.7 %copy-start.32 = (bf16[1024,1536]{1,0:T(8,128)(2,1)S(1)}, bf16[1024,1536]{1,0:T(8,128)(2,1)}, u32[]{:S(2)}) copy-start(bf16[1024,1536]{1,0:T(8,128)(2,1)} %get-tuple-element.64) | copy-start | bytes 9437188
  301.5 4.8 copy-start.17
  301.5 4.8 copy-start.30
  306.3 3.0 copy-start.28
  325.0 5.6 copy-start.26
  325.0 5.6 copy-start.31
  325.0 12.7 %slice-start = ((s8[4718592]{0:T(1024)(128)(4,1)}), s8[4194304]{0:T(1024)(128)(4,1)S(1)}, s32[]{:S(2)}) async-start(s8[4718592]{0:T(1024)(128)(4,1)} %bitcast.158), calls=%async_computation.5 | async-start | bytes 8388608
  330.6 7.2 %slice-start.1 = ((s8[4718592]{0:T(1024)(128)(4,1)}), s8[524288]{0:T(1024)(128)(4,1)S(1)}, s32[]{:S(2)}) async-start(s8[4718592]{0:T(1024)(128)(4,1)} %bitcast.158), calls=%async_computation.6 | async-start | bytes 1048576
  336.3 5.2 copy-start.4
  336.3 5.2 copy-start.8
  336.3 82.9 %collective-permute-start.3 = (bf16[512,768]{1,0:T(8,128)(2,1)}, bf16[512,768]{1,0:T(8,128)(2,1)}, u32[]{:S(2)}, u32[]{:S(2)}) collective-permute-start(bf16[512,768]{1,0:T(8,128)(2,1)} %get-tuple-element.43), channel_id=1, source_target_pairs={{0,1},{1,0},{2,3},{3,2},{4,5},{5,4},{6,7},{7,6},{8,9},{9,8},{10,11... | collective-permute-start | bytes 2359304 | tf_op jit(solution)/shard_map/ppermute | solution.py:290
  341.5 4.9 copy-start.1
  346.4 4.3 copy-start.24
  350.1 71.9 %collective-permute-start.5 = (bf16[512,768]{1,0:T(8,128)(2,1)}, bf16[512,768]{1,0:T(8,128)(2,1)}, u32[]{:S(2)}, u32[]{:S(2)}) collective-permute-start(bf16[512,768]{1,0:T(8,128)(2,1)} %fusion.46), channel_id=1, source_target_pairs={{0,1},{1,0},{2,3},{3,2},{4,5},{5,4},{6,7},{7,6},{8,9},{9,8},{10,11... | collective-permute-start | bytes 2359304 | tf_op jit(solution)/shard_map/ppermute | solution.py:290
  417.8 1.5 copy-start.13
Sparse Core Ops, SparseCore 0:
  11.5 117.2 all-gather.1
  295.9 114.5 reduce-scatter.2
  416.4 135.2 reduce-scatter.4

commit v2 on v1

--- a/solution.py
+++ b/solution.py
@@ -145,6 +145,17 @@
         sums_ref[i : i + 1, :] += sums[i]
 
 
+def sum_by_pairs(vector, axes):
+    for axis in axes:
+        size = lax.axis_size(axis)
+        assert size & (size - 1) == 0
+        step = 1
+        while step < size:
+            vector = vector + lax.ppermute(vector, axis, [(i, i ^ step) for i in range(size)])
+            step *= 2
+    return vector
+
+
 def attend(normed, weight, bias, query_gain, query_bias, key_gain, ids, local_width):
     length, width = normed.shape
     tp = weight.shape[0]
@@ -351,15 +362,22 @@
         terms_up.append(mm_tn(normed2, grad_preact).astype(BF))
         terms_down.append(mm_tn(grad_low, hidden[i]).astype(BF))
         sums_up.append(jnp.sum(grad_preact.astype(F32), axis=0))
-    late = jnp.stack(
-        [jnp.concatenate([terms_up[i], terms_down[i]], axis=1) for i in range(tp)]
-    ).reshape(tp * width, -1)
-    late = lax.psum_scatter(late, everyone, scatter_dimension=0, tiled=True).astype(F32)
-    up_weight_grad = late[:, :local_hidden]
-    down_weight_grad = late[:, local_hidden:].T
-
     grad_resid = grad_y + norm_back(grad_normed2, unit_two, scaled_two, norm2_gain)
     grad_resr = grad_resid.astype(BF)
+    terms_out = [
+        mm_tn(grad_resr, mixed[:, i * local_width : (i + 1) * local_width]).astype(BF)
+        for i in range(tp)
+    ]
+    late = jnp.stack(
+        [jnp.concatenate([terms_up[i], terms_down[i], terms_out[i]], axis=1) for i in range(tp)]
+    ).reshape(tp * width, -1)
+    late, grad_resr = lax.optimization_barrier((late, grad_resr))
+    late = lax.psum_scatter(late, everyone, scatter_dimension=0, tiled=True)
+    late = late.astype(F32)
+    up_weight_grad = late[:, :local_hidden]
+    down_weight_grad = late[:, local_hidden : 2 * local_hidden].T
+    out_weight_grad = late[:, 2 * local_hidden :].T
+
     grad_project, head_sums = attend_back(
         grad_resr,
         gathered,
@@ -372,26 +390,22 @@
         local_width,
     )
     grad_normed1 = 0.0
-    terms_qkv, terms_out, sums_qkv = [], [], []
+    terms_qkv, sums_qkv = [], []
+    for i in range(tp):
+        terms_qkv.append(mm_tn(normed1, grad_project[i]).astype(BF))
+        sums_qkv.append(jnp.sum(grad_project[i].astype(F32), axis=0))
+    early = jnp.stack(terms_qkv)
+    early, grad_project = lax.optimization_barrier((early, grad_project))
+    theirs = lax.ppermute(pick(early, 1 - me), "tp", swap)
+    early = (pick(early, me).astype(F32) + theirs.astype(F32)).astype(BF)
+    early = lax.psum_scatter(early, "fsdp", scatter_dimension=0, tiled=True).astype(F32)
     for i in range(tp):
         grad_normed1 = grad_normed1 + mm_nt(grad_project[i], qkv[i])
-        terms_qkv.append(mm_tn(normed1, grad_project[i]).astype(BF))
-        terms_out.append(
-            mm_tn(grad_resr, mixed[:, i * local_width : (i + 1) * local_width]).astype(BF)
-        )
-        sums_qkv.append(jnp.sum(grad_project[i].astype(F32), axis=0))
-    early = jnp.stack(
-        [jnp.concatenate([terms_qkv[i], terms_out[i]], axis=1) for i in range(tp)]
-    ).reshape(tp * width, -1)
-    early = lax.psum_scatter(early, everyone, scatter_dimension=0, tiled=True).astype(F32)
     qkv_weight_grad = (
-        early[:, :edge_out]
-        .reshape(shard, per, 3, lanes)
+        early.reshape(shard, per, 3, lanes)
         .transpose(0, 2, 1, 3)
         .reshape(qkv_weight.shape)
     )
-    out_weight_grad = early[:, edge_out:].T
-
     input_grad = grad_resid + norm_back(grad_normed1, unit_one, scaled_one, norm1_gain)
     input_grad = from_sequence(input_grad, BF)
 
@@ -408,7 +422,7 @@
         *sums_qkv,
         *sums_up,
     ]
-    summed = lax.psum(jnp.concatenate(vectors), everyone)
+    summed = sum_by_pairs(jnp.concatenate(vectors), everyone)
     pieces, start = [], 0
     for vector in vectors:
         pieces.append(summed[start : start + vector.shape[0]])

time: 565 us -> 587 us (1.039)
  waiting for transfers between devices: 226 us -> 302 us
  blocking collectives: 65 us -> 0 us
  starting transfers between devices: 7.26 us -> 13.9 us
  other arithmetic: 40.4 us -> 34 us
  matrix products: 79.8 us -> 85.9 us
    psum x1 -> x0, blocking collectives: 65 us -> none  [on_device(): summed = lax.psum(jnp.concatenate(vectors), everyone)]
    ppermute x0 -> x6, waiting for transfers between devices: none -> 45.9 us  [the longest x1 39.3 us: on_device(): theirs = lax.ppermute(pick(early, 1 - me), 'tp', swap)]
    ppermute x2, waiting for transfers between devices: 0.01 us -> 27.5 us  [from_sequence(): lax.ppermute(pick(halves, 1 - me).astype(dtype), 'tp', swap)]
    another operation x5 -> x4, other arithmetic: 15.6 us -> 6.02 us  [the longest x3 5.66 us: on_device(): jnp.stack([jnp.concatenate([terms_up[i], terms_down[i], terms_out[i]], ax...]
    ppermute x0 -> x6, starting transfers between devices: none -> 6.6 us  [the longest x5 5.12 us: sum_by_pairs(): lax.ppermute(vector, axis, [(i, i ^ step) for i in range(size)])]
  transfers between devices with their start and end apart: 9 -> 15, of which waited for: 3 -> 8; matrix products, arithmetic and copies ran while one was open for 17% -> 11% of each run, Pallas kernels for 7% -> 7%
where the time goes in v2:
time: 587 us; the launch traced here: 583 us
  waiting for transfers between devices  302 us (51%)
  Pallas kernels  111 us (19%)
  matrix products  85.9 us (15%)
  other arithmetic  34 us (6%)
  local copies, waits for them, and re-layouts  21.6 us (4%)
  between operations  14.7 us (3%)
  starting transfers between devices  13.9 us (2%)
    reduce_scatter x1, waiting for transfers between devices, on_device(): late = lax.psum_scatter(late, everyone, scatter_dimension=0, tiled=True)  125 us
    all_gather x1, waiting for transfers between devices, on_device(): lax.all_gather(packed, everyone, axis=0, tiled=True).reshape(tp, width, -1)  84.9 us
    pallas_call x1, Pallas kernels, attend_back(): pl.pallas_call(partial(attend_back_kernel, depth=depth), grid=(tp * per,)...  69 us
    pallas_call x1, Pallas kernels, attend(): pl.pallas_call(partial(attend_kernel, depth=depth), grid=(tp * per,), in_...  42 us
    ppermute x1, waiting for transfers between devices, on_device(): theirs = lax.ppermute(pick(early, 1 - me), 'tp', swap)  39.3 us
    dot_general x8, matrix products, mm_nt(): lax.dot_general(a, b, (((1,), (1,)), ((), ())), preferred_element_type=F32)  35.5 us
    ppermute x2, waiting for transfers between devices, from_sequence(): lax.ppermute(pick(halves, 1 - me).astype(dtype), 'tp', swap)  27.5 us
    dot_general x4, matrix products, mm(): return jnp.dot(a, b, preferred_element_type=F32)  26.9 us
  transfers between devices with their start and end apart: 15, of which 8 were waited for; matrix products, arithmetic and copies ran while one was open for 11% of the time, Pallas kernels for 7%

profile of v2, /device:TPU:0, one launch (start us, length us, event | category | flops | bytes accessed | tf_op | source)
XLA Modules:
  0.0 583.2 jit_solution(14005821582039128661)
XLA Ops:
  8.5 1.8 pad_maximum_fusion.2
  11.1 3.0 collective-permute-start.2
  16.7 2.0 collective-permute-start
  18.7 1.2 dynamic-slice_bitcast_fusion.2
  22.7 17.7 %collective-permute-done = bf16[512,768]{1,0:T(8,128)(2,1)S(1)} collective-permute-done((bf16[512,768]{1,0:T(8,128)(2,1)}, bf16[512,768]{1,0:T(8,128)(2,1)S(1)}, u32[]{:S(2)}, u32[]{:S(2)}) %collective-permute-start) | collective-permute-done | bytes 786464 | tf_op jit(solution)/shard_map/ppermute | solution.py:297
  41.7 3.1 fusion.18.x_ref
  44.8 84.9 %all-gather.2.cloned.1.call-done = bf16[1536,4608]{1,0:T(8,128)(2,1)} async-done(((bf16[48,4608]{1,0:T(8,128)(2,1)}), bf16[1536,4608]{1,0:T(8,128)(2,1)}) %all-gather.2.cloned.1.call-update) | async-done | bytes 14155792 | tf_op jit(solution)/shard_map/all_gather | solution.py:314
  129.7 42.0 %attend.1 = (f32[2,1024,1152]{2,1,0:T(8,128)}, bf16[1024,768]{1,0:T(8,128)(2,1)}) custom-call(bf16[1024,768]{1,0:T(8,128)(2,1)} %fusion.18.x_ref, bf16[2,768,4608]{2,1,0:T(8,128)(2,1)} %bitcast.147, f32[2,1,1152]{2,1,0:T(1,128)} %broadcast_in_dim.14.b_ref, f32[1,64]{1,0:T(1,128)} %bitcast.176, f32[1,64]{1,0:T(1,128)} %bitcast.178, f32[1,64]{1,0:T(1,128)} %bitcast.180, ...), custom_call_target="tpu_custom_call" | custom-call | flops 3623878656 | bytes 12582912 | tf_op jit(solution)/shard_map/attend/pallas_call | solution.py:166
  171.7 2.5 fusion.53
  174.2 2.5 fusion.58
  179.4 5.4 multiply_convert_fusion.3
  184.8 8.0 %convert_reduce_fusion.1 = (f32[1536]{0:T(1024)S(1)}, bf16[1024,1536]{1,0:T(8,128)(2,1)S(1)}) fusion(f32[1024,1536]{1,0:T(8,128)} %get-tuple-element.73, f32[1536]{0:T(1024)S(1)} %get-tuple-element.44, bf16[2,768,4608]{2,1,0:T(8,128)(2,1)S(1)} %bitcast.156, bf16[512,768]{1,0:T(8,128)(2,1)} %collective-permute-done.4, bf16[512,768]{1,0:T(8,128)(2,1)S(1)} %copy-done.13, ...), kind=kOutput, calls=%fused_computation.14 | convolution fusion | flops 2446588416 | bytes 13383681 | tf_op jit(solution)/shard_map/dot_general | solution.py:35
  192.8 3.0 convolution_convert_fusion.3
  195.8 4.3 fusion.37
  200.2 5.6 multiply_convert_fusion.2
  205.8 7.8 %convert_reduce_fusion = (f32[1536]{0:T(1024)S(1)}, bf16[1024,1536]{1,0:T(8,128)(2,1)S(1)}) fusion(f32[1024,1536]{1,0:T(8,128)} %get-tuple-element.75, f32[1536]{0:T(1024)S(1)} %get-tuple-element.43, bf16[2,768,4608]{2,1,0:T(8,128)(2,1)S(1)} %bitcast.159, bf16[512,768]{1,0:T(8,128)(2,1)} %collective-permute-done.4, bf16[512,768]{1,0:T(8,128)(2,1)S(1)} %copy-done.13, ...), kind=kOutput, calls=%fused_computation.13 | convolution fusion | flops 2446588416 | bytes 13383681 | tf_op jit(solution)/shard_map/dot_general | solution.py:35
  213.6 3.4 convolution_convert_fusion.1
  217.0 5.2 multiply_reduce_fusion
  222.2 3.9 fusion.55
  226.3 2.4 copy-done.19
  231.7 4.4 convolution_convert_fusion.2
  236.6 1.4 copy-done.28
  238.1 4.4 convolution_convert_fusion
  242.9 4.8 pad_maximum_fusion
  247.7 69.0 %attend_back.1 = (bf16[2,1024,1152]{2,1,0:T(8,128)(2,1)}, f32[3,64]{1,0:T(4,128)}) custom-call(bf16[1024,768]{1,0:T(8,128)(2,1)} %copy-done.11, bf16[2,768,4608]{2,1,0:T(8,128)(2,1)} %bitcast.150, f32[2,1024,1152]{2,1,0:T(8,128)} %get-tuple-element.27.p_ref, f32[1,64]{1,0:T(1,128)} %bitcast.177, f32[1,64]{1,0:T(1,128)} %bitcast.179, f32[1,64]{1,0:T(1,128)} %bitcast.181, ...), custom_call_target="tpu_custom_call" | custom-call | flops 4831838208 | bytes 14155776 | tf_op jit(solution)/shard_map/attend_back/pallas_call | solution.py:216
  316.8 4.1 fusion.28
  320.9 2.3 fusion.27
  323.7 1.5 collective-permute-start.11
  325.1 39.3 %collective-permute-done.11 = bf16[768,1152]{1,0:T(8,128)(2,1)S(1)} collective-permute-done((bf16[768,1152]{1,0:T(8,128)(2,1)S(1)}, bf16[768,1152]{1,0:T(8,128)(2,1)S(1)}, u32[]{:S(2)}, u32[]{:S(2)}) %collective-permute-start.11) | collective-permute-done | bytes 1769504 | tf_op jit(solution)/shard_map/ppermute | solution.py:399
  364.5 1.7 fusion.16
  367.0 3.3 convert_reduce_fusion.3
  370.3 4.7 fusion.29
  375.0 6.3 %fusion.23 = (f32[768]{0:T(1024)S(1)}, f32[1024]{0:T(1024)S(1)}, f32[1024]{0:T(1024)S(1)}, f32[768]{0:T(1024)S(1)}, f32[1024,768]{1,0:T(8,128)}) fusion(f32[1024]{0:T(1024)S(1)} %add_rsqrt_fusion.1, f32[1024]{0:T(1024)S(1)} %broadcast_multiply_fusion.5, bf16[512,768]{1,0:T(8,128)(2,1)S(1)} %copy-done.4, bf16[512,768]{1,0:T(8,128)(2,1)S(1)} %copy-done.9, ...), kind=kOutput, calls=%fused_computation.51 | convolution fusion | flops 1827664384 | bytes 12019713 | tf_op jit(solution)/shard_map/dot_general | solution.py:39
  381.4 1.4 collective-permute-start.6
  382.9 5.4 fusion.39
  388.3 4.5 add_convert_fusion
  393.0 2.5 fusion.22
  396.3 3.3 collective-permute-done.8
  400.7 3.2 collective-permute-done.9
  403.9 2.0 collective-permute-start.10
  406.9 1.2 collective-permute-start.3
  411.5 16.1 %collective-permute-done.3 = bf16[512,768]{1,0:T(8,128)(2,1)} collective-permute-done((bf16[512,768]{1,0:T(8,128)(2,1)}, bf16[512,768]{1,0:T(8,128)(2,1)}, u32[]{:S(2)}, u32[]{:S(2)}) %collective-permute-start.3) | collective-permute-done | bytes 786464 | tf_op jit(solution)/shard_map/ppermute | solution.py:301
  427.6 2.9 maximum_select_fusion.2
  430.5 11.4 %collective-permute-done.5 = bf16[512,768]{1,0:T(8,128)(2,1)} collective-permute-done((bf16[512,768]{1,0:T(8,128)(2,1)S(1)}, bf16[512,768]{1,0:T(8,128)(2,1)}, u32[]{:S(2)}, u32[]{:S(2)}) %collective-permute-start.5) | collective-permute-done | bytes 786464 | tf_op jit(solution)/shard_map/ppermute | solution.py:301
  441.9 1.3 bitcast_convert_fusion
  443.2 1.9 maximum_select_fusion
  447.0 125.5 %reduce-scatter.5.cloned.1.call-done = bf16[48,3456]{1,0:T(8,128)(2,1)} async-done(((bf16[1536,3456]{1,0:T(8,128)(2,1)}), bf16[48,3456]{1,0:T(8,128)(2,1)}) %reduce-scatter.5.cloned.1.call-update) | async-done | bytes 331792 | tf_op jit(solution)/shard_map/reduce_scatter | solution.py:375
  574.8 1.6 slice.173
  (141 shorter events, 27.5 us)
Async XLA Ops:
  7.2 8.5 %copy-start.15 = (bf16[2,512,768]{2,1,0:T(8,128)(2,1)S(1)}, bf16[2,512,768]{2,1,0:T(8,128)(2,1)}, u32[]{:S(2)}) copy-start(bf16[2,512,768]{2,1,0:T(8,128)(2,1)} %param.18) | copy-start | bytes 4718596
  7.2 122.5 %all-gather.2.cloned.1.call-start = ((), (), s32[]{:S(2)}) async-start(), calls=%async_computation.2 | async-start | bytes 14598144 | tf_op jit(solution)/shard_map/all_gather | solution.py:314
  10.3 434.8 %reduce-scatter.3.cloned.1.call-start = ((), (), s32[]{:S(2)}) async-start(), calls=%async_computation.3 | async-start | bytes 1880064 | tf_op jit(solution)/shard_map/reduce_scatter | solution.py:401
  11.1 8.9 %collective-permute-start.2 = (s32[512]{0:T(512)S(1)}, s32[512]{0:T(512)S(1)}, u32[]{:S(2)}, u32[]{:S(2)}) collective-permute-start(s32[512]{0:T(512)S(1)} %bitcast.175), channel_id=1, source_target_pairs={{0,1},{1,0},{2,3},{3,2},{4,5},{5,4},{6,7},{7,6},{8,9},{9,8},{10,11... | collective-permute-start | bytes 6152 | tf_op jit(solution)/shard_map/ppermute | solution.py:297
  14.8 3.8 copy-start.16
  15.6 6.4 %collective-permute-start.1 = (f32[2688]{0:T(1024)S(1)}, f32[2688]{0:T(1024)S(1)}, u32[]{:S(2)}, u32[]{:S(2)}) collective-permute-start(f32[2688]{0:T(1024)S(1)} %constant_dynamic-update-slice_fusion), channel_id=1, source_target_pairs={{0,1},{1,0},{2,3},{3,2},{4,5},{5,4},{6,7},{7,6},{8,9},{9,8},{10,11... | collective-permute-start | bytes 32264 | tf_op jit(solution)/shard_map/ppermute | solution.py:326
  16.6 25.0 %copy-start.2 = (bf16[512,768]{1,0:T(8,128)(2,1)}, bf16[512,768]{1,0:T(8,128)(2,1)S(1)}, u32[]{:S(2)}) copy-start(bf16[512,768]{1,0:T(8,128)(2,1)S(1)} %get-tuple-element.53) | copy-start | bytes 2359300
  16.7 23.8 %collective-permute-start = (bf16[512,768]{1,0:T(8,128)(2,1)}, bf16[512,768]{1,0:T(8,128)(2,1)S(1)}, u32[]{:S(2)}, u32[]{:S(2)}) collective-permute-start(bf16[512,768]{1,0:T(8,128)(2,1)} %get-tuple-element.52), channel_id=1, source_target_pairs={{0,1},{1,0},{2,3},{3,2},{4,5},{5,4},{6,7},{7,6},{8,9},{9,8},{10,11... | collective-permute-start | bytes 2359304 | tf_op jit(solution)/shard_map/ppermute | solution.py:297
  19.9 21.8 %copy-start.20 = (f32[768]{0:T(1024)S(1)}, f32[768]{0:T(1024)}, u32[]{:S(2)}) copy-start(f32[768]{0:T(1024)} %param.21) | copy-start | bytes 9220
  19.9 21.8 %copy-start.22 = (f32[768]{0:T(1024)S(1)}, f32[768]{0:T(1024)}, u32[]{:S(2)}) copy-start(f32[768]{0:T(1024)} %param.22) | copy-start | bytes 9220
  19.9 164.9 %collective-permute-start.4 = (bf16[512,768]{1,0:T(8,128)(2,1)}, bf16[512,768]{1,0:T(8,128)(2,1)}, u32[]{:S(2)}, u32[]{:S(2)}) collective-permute-start(bf16[512,768]{1,0:T(8,128)(2,1)} %get-tuple-element.49), channel_id=1, source_target_pairs={{0,1},{1,0},{2,3},{3,2},{4,5},{5,4},{6,7},{7,6},{8,9},{9,8},{10,11... | collective-permute-start | bytes 2359304 | tf_op jit(solution)/shard_map/ppermute | solution.py:297
  40.4 4.4 copy-start.7
  171.6 2.5 copy-start.3
  171.6 2.5 copy-start.8
  171.6 2.5 copy-start.18
  171.7 2.5 copy-start.25
  174.2 5.2 copy-start.6
  176.7 1.4 copy-start.21
  176.7 1.5 copy-start.23
  179.4 5.4 copy-start.13
  226.1 3.6 copy-start
  226.1 2.5 copy-start.19
  228.7 1.2 copy-start.11
  229.8 1.9 copy-start.27
  236.2 1.9 copy-start.28
  247.7 69.0 %copy-start.17 = (bf16[1024,768]{1,0:T(8,128)(2,1)S(1)}, bf16[1024,768]{1,0:T(8,128)(2,1)}, u32[]{:S(2)}) copy-start(bf16[1024,768]{1,0:T(8,128)(2,1)} %fusion.18.x_ref) | copy-start | bytes 4718596
  316.8 4.1 copy-start.12
  323.7 40.8 %collective-permute-start.11 = (bf16[768,1152]{1,0:T(8,128)(2,1)S(1)}, bf16[768,1152]{1,0:T(8,128)(2,1)S(1)}, u32[]{:S(2)}, u32[]{:S(2)}) collective-permute-start(bf16[768,1152]{1,0:T(8,128)(2,1)S(1)} %dynamic-slice_bitcast_fusion), channel_id=1, source_target_pairs={{0,1},{1,0},{2,3},{3,2},{4,5},{5,4},{6,7},{7,6},{8,9},{9,8},{10,11... | collective-permute-start | bytes 5308424 | tf_op jit(solution)/shard_map/ppermute | solution.py:399
  366.2 0.8 copy-start.24
  366.2 206.2 %reduce-scatter.5.cloned.1.call-start = ((), (), s32[]{:S(2)}) async-start(), calls=%async_computation.4 | async-start | bytes 10948608 | tf_op jit(solution)/shard_map/reduce_scatter | solution.py:375
  367.0 8.0 %slice-start = ((s8[4718592]{0:T(1024)(128)(4,1)}), s8[4194304]{0:T(1024)(128)(4,1)S(1)}, s32[]{:S(2)}) async-start(s8[4718592]{0:T(1024)(128)(4,1)} %bitcast.163), calls=%async_computation.5 | async-start | bytes 8388608
  370.3 4.7 copy-start.4
  370.3 4.7 copy-start.9
  370.3 4.7 slice-start.1
  381.4 11.5 %collective-permute-start.6 = (f32[10176]{0:T(1024)S(1)}, f32[10176]{0:T(1024)S(1)}, u32[]{:S(2)}, u32[]{:S(2)}) collective-permute-start(f32[10176]{0:T(1024)S(1)} %concatenate.94), channel_id=1, source_target_pairs={{0,1},{1,0},{2,3},{3,2},{4,5},{5,4},{6,7},{7,6},{8,9},{9,8},{10,11... | collective-permute-start | bytes 122120 | tf_op jit(solution)/shard_map/ppermute | solution.py:154
  382.9 5.4 copy-start.26
  382.9 5.4 copy-start.29
  388.3 4.7 copy-start.1
  388.3 4.7 copy-start.5
  388.3 4.7 copy-start.10
  388.3 4.7 copy-start.14
  392.9 2.6 collective-permute-start.7
  395.6 4.1 collective-permute-start.8
  399.6 4.3 collective-permute-start.9
  403.9 5.0 collective-permute-start.10
  406.9 20.7 %collective-permute-start.3 = (bf16[512,768]{1,0:T(8,128)(2,1)}, bf16[512,768]{1,0:T(8,128)(2,1)}, u32[]{:S(2)}, u32[]{:S(2)}) collective-permute-start(bf16[512,768]{1,0:T(8,128)(2,1)} %get-tuple-element.51), channel_id=1, source_target_pairs={{0,1},{1,0},{2,3},{3,2},{4,5},{5,4},{6,7},{7,6},{8,9},{9,8},{10,11... | collective-permute-start | bytes 2359304 | tf_op jit(solution)/shard_map/ppermute | solution.py:301
  408.0 33.9 %collective-permute-start.5 = (bf16[512,768]{1,0:T(8,128)(2,1)S(1)}, bf16[512,768]{1,0:T(8,128)(2,1)}, u32[]{:S(2)}, u32[]{:S(2)}) collective-permute-start(bf16[512,768]{1,0:T(8,128)(2,1)S(1)} %fusion.49), channel_id=1, source_target_pairs={{0,1},{1,0},{2,3},{3,2},{4,5},{5,4},{6,7},{7,6},{8,9},{9,8},{10,11... | collective-permute-start | bytes 2359304 | tf_op jit(solution)/shard_map/ppermute | solution.py:301
Sparse Core Ops, SparseCore 0:
  11.5 118.1 all-gather.1
  366.3 58.9 reduce-scatter.2
  431.4 140.9 reduce-scatter.4

commit v3 on v2

--- a/solution.py
+++ b/solution.py
@@ -145,6 +145,20 @@
         sums_ref[i : i + 1, :] += sums[i]
 
 
+def add_halves(own, other):
+    return (own.astype(F32) + other.astype(F32)).astype(BF)
+
+
+def halve_over_fsdp(array, step):
+    size = lax.axis_size("fsdp")
+    assert size & (size - 1) == 0
+    bit = lax.axis_index("fsdp") // step % 2
+    pairs = array.reshape(array.shape[0], -1, 2, *array.shape[2:])
+    own = lax.dynamic_index_in_dim(pairs, bit, 2, keepdims=False)
+    other = lax.dynamic_index_in_dim(pairs, 1 - bit, 2, keepdims=False)
+    return add_halves(own, lax.ppermute(other, "fsdp", [(i, i ^ step) for i in range(size)]))
+
+
 def sum_by_pairs(vector, axes):
     for axis in axes:
         size = lax.axis_size(axis)
@@ -343,7 +357,6 @@
     unit_two, scaled_two = norm_parts(resid)
     normed2 = (unit_two * norm2_gain + norm2_bias).astype(BF)
 
-    output = resid + down_bias
     hidden, slope = [], []
     for i in range(tp):
         preact = mm(normed2, up[i]) + up_bias_all[i]
@@ -351,8 +364,6 @@
         bell = jnp.exp(-0.5 * preact * preact) * ((0.5 / jnp.pi) ** 0.5)
         hidden.append((preact * half).astype(BF))
         slope.append((half + preact * bell).astype(BF))
-        output = output + mm_nt(hidden[i], down_t[i])
-    output = from_sequence(output.astype(BF), BF)
 
     grad_normed2 = 0.0
     terms_up, terms_down, sums_up = [], [], []
@@ -371,7 +382,7 @@
     late = jnp.stack(
         [jnp.concatenate([terms_up[i], terms_down[i], terms_out[i]], axis=1) for i in range(tp)]
     ).reshape(tp * width, -1)
-    late, grad_resr = lax.optimization_barrier((late, grad_resr))
+    late, grad_resr, hidden = lax.optimization_barrier((late, grad_resr, hidden))
     late = lax.psum_scatter(late, everyone, scatter_dimension=0, tiled=True)
     late = late.astype(F32)
     up_weight_grad = late[:, :local_hidden]
@@ -389,6 +400,11 @@
         ids,
         local_width,
     )
+    output = resid + down_bias
+    for i in range(tp):
+        output = output + mm_nt(hidden[i], down_t[i])
+    output = from_sequence(output.astype(BF), BF)
+
     grad_normed1 = 0.0
     terms_qkv, sums_qkv = [], []
     for i in range(tp):
@@ -396,9 +412,16 @@
         sums_qkv.append(jnp.sum(grad_project[i].astype(F32), axis=0))
     early = jnp.stack(terms_qkv)
     early, grad_project = lax.optimization_barrier((early, grad_project))
-    theirs = lax.ppermute(pick(early, 1 - me), "tp", swap)
-    early = (pick(early, me).astype(F32) + theirs.astype(F32)).astype(BF)
-    early = lax.psum_scatter(early, "fsdp", scatter_dimension=0, tiled=True).astype(F32)
+    early = early.reshape(tp, -1, shard, edge_out)
+    early = halve_over_fsdp(early, 1)
+    early = add_halves(
+        pick(early, me), lax.ppermute(pick(early, 1 - me), "tp", swap)
+    )[None]
+    step = 2
+    while step < lax.axis_size("fsdp"):
+        early = halve_over_fsdp(early, step)
+        step *= 2
+    early = early.reshape(shard, edge_out).astype(F32)
     for i in range(tp):
         grad_normed1 = grad_normed1 + mm_nt(grad_project[i], qkv[i])
     qkv_weight_grad = (

time: 587 us -> 426 us (0.73)
  waiting for transfers between devices: 302 us -> 139 us
    reduce_scatter x1, waiting for transfers between devices: 125 us -> 0.01 us  [on_device(): late = lax.psum_scatter(late, everyone, scatter_dimension=0, tiled=True)]
    ppermute x2, waiting for transfers between devices: 27.5 us -> 0.01 us  [from_sequence(): lax.ppermute(pick(halves, 1 - me).astype(dtype), 'tp', swap)]
    ppermute x1 -> x5, waiting for transfers between devices: 39.3 us -> 32.2 us  [the longest x1 20.1 us: on_device(): lax.ppermute(pick(early, 1 - me), 'tp', swap)]
  transfers between devices with their start and end apart: 15 -> 18, of which waited for: 8 -> 8; matrix products, arithmetic and copies ran while one was open for 11% -> 17% of each run, Pallas kernels for 7% -> 26%
where the time goes in v3:
time: 426 us; the launch traced here: 422 us
  waiting for transfers between devices  139 us (33%)
  Pallas kernels  111 us (26%)
  matrix products  83.2 us (20%)
  other arithmetic  34.9 us (8%)
  local copies, waits for them, and re-layouts  22.4 us (5%)
  starting transfers between devices  16.4 us (4%)
  between operations  15.2 us (4%)
    all_gather x1, waiting for transfers between devices, on_device(): lax.all_gather(packed, everyone, axis=0, tiled=True).reshape(tp, width, -1)  83 us
    pallas_call x1, Pallas kernels, attend_back(): pl.pallas_call(partial(attend_back_kernel, depth=depth), grid=(tp * per,)...  69.1 us
    pallas_call x1, Pallas kernels, attend(): pl.pallas_call(partial(attend_kernel, depth=depth), grid=(tp * per,), in_...  41.9 us
    dot_general x8, matrix products, mm_nt(): lax.dot_general(a, b, (((1,), (1,)), ((), ())), preferred_element_type=F32)  34.1 us
    dot_general x4, matrix products, mm(): return jnp.dot(a, b, preferred_element_type=F32)  25.6 us
    dot_general x8, matrix products, mm_tn(): lax.dot_general(a, b, (((0,), (0,)), ((), ())), preferred_element_type=F32)  23.6 us
    ppermute x1, waiting for transfers between devices, on_device(): lax.ppermute(pick(early, 1 - me), 'tp', swap)  20.1 us
    ppermute x3, waiting for transfers between devices, to_sequence(): lax.ppermute(pick(array, 1 - me), 'tp', swap)  16.9 us
  transfers between devices with their start and end apart: 18, of which 8 were waited for; matrix products, arithmetic and copies ran while one was open for 17% of the time, Pallas kernels for 26%

profile of v3, /device:TPU:0, one launch (start us, length us, event | category | flops | bytes accessed | tf_op | source)
XLA Modules:
  0.0 422.3 jit_solution(10954710092189333504)
XLA Ops:
  8.5 1.8 pad_maximum_fusion.2
  11.4 3.0 collective-permute-start
  14.5 2.0 collective-permute-start.1
  16.6 2.6 dynamic-slice_bitcast_fusion.4
  19.2 16.9 %collective-permute-done.2 = s32[512]{0:T(512)S(1)} collective-permute-done((s32[512]{0:T(512)S(1)}, s32[512]{0:T(512)S(1)}, u32[]{:S(2)}, u32[]{:S(2)}) %collective-permute-start.2) | collective-permute-done | bytes 2080 | tf_op jit(solution)/shard_map/ppermute | solution.py:311
  40.1 3.1 fusion.18.x_ref
  43.2 83.0 %all-gather.2.cloned.1.call-done = bf16[1536,4608]{1,0:T(8,128)(2,1)} async-done(((bf16[48,4608]{1,0:T(8,128)(2,1)}), bf16[1536,4608]{1,0:T(8,128)(2,1)}) %all-gather.2.cloned.1.call-update) | async-done | bytes 14155792 | tf_op jit(solution)/shard_map/all_gather | solution.py:328
  126.2 41.9 %attend.1 = (f32[2,1024,1152]{2,1,0:T(8,128)}, bf16[1024,768]{1,0:T(8,128)(2,1)}) custom-call(bf16[1024,768]{1,0:T(8,128)(2,1)} %fusion.18.x_ref, bf16[2,768,4608]{2,1,0:T(8,128)(2,1)} %bitcast.169, f32[2,1,1152]{2,1,0:T(1,128)} %broadcast_in_dim.14.b_ref, f32[1,64]{1,0:T(1,128)} %bitcast.202, f32[1,64]{1,0:T(1,128)} %bitcast.204, f32[1,64]{1,0:T(1,128)} %bitcast.206, ...), custom_call_target="tpu_custom_call" | custom-call | flops 3623878656 | bytes 12582912 | tf_op jit(solution)/shard_map/attend/pallas_call | solution.py:180
  168.2 2.5 fusion.55
  170.7 2.6 fusion.62
  175.9 5.1 %multiply_convert_fusion.2 = (bf16[1024,1536]{1,0:T(8,128)(2,1)}, f32[1024,1536]{1,0:T(8,128)S(1)}) fusion(f32[1536]{0:T(1024)S(1)} %get-tuple-element.48, bf16[1024,768]{1,0:T(8,128)(2,1)S(1)} %add_convert_fusion.1, bf16[2,768,4608]{2,1,0:T(8,128)(2,1)S(1)} %bitcast.177), kind=kOutput, calls=%fused_computation.18 | convolution fusion | flops 2425356288 | bytes 13377536 | tf_op jit(solution)/shard_map/dot_general | solution.py:35
  181.1 7.0 %convert_reduce_fusion.1 = (f32[1536]{0:T(1024)S(1)}, bf16[1024,1536]{1,0:T(8,128)(2,1)S(1)}) fusion(f32[1024,1536]{1,0:T(8,128)S(1)} %get-tuple-element.80, f32[1536]{0:T(1024)S(1)} %get-tuple-element.48, bf16[2,768,4608]{2,1,0:T(8,128)(2,1)S(1)} %bitcast.178, bf16[512,768]{1,0:T(8,128)(2,1)} %collective-permute-done.3, ...), kind=kOutput, calls=%fused_computation.14 | convolution fusion | flops 2446588416 | bytes 13383681 | tf_op jit(solution)/shard_map/dot_general | solution.py:35
  188.1 4.3 %fusion.38 = f32[1024,768]{1,0:T(8,128)} fusion(bf16[1024,1536]{1,0:T(8,128)(2,1)S(1)} %get-tuple-element.83, bf16[2,768,4608]{2,1,0:T(8,128)(2,1)S(1)} %bitcast.179), kind=kOutput, calls=%fused_computation.79 | convolution fusion | flops 2415919104 | bytes 8650752 | tf_op jit(solution)/shard_map/dot_general | solution.py:39
  192.4 3.0 convolution_convert_fusion.3
  195.4 5.7 %multiply_convert_fusion = (bf16[1024,1536]{1,0:T(8,128)(2,1)}, f32[1024,1536]{1,0:T(8,128)}) fusion(f32[1536]{0:T(1024)S(1)} %get-tuple-element.47, bf16[1024,768]{1,0:T(8,128)(2,1)S(1)} %add_convert_fusion.1, bf16[2,768,4608]{2,1,0:T(8,128)(2,1)S(1)} %bitcast.180), kind=kOutput, calls=%fused_computation.15 | convolution fusion | flops 2425356288 | bytes 13377536 | tf_op jit(solution)/shard_map/dot_general | solution.py:35
  201.1 7.8 %convert_reduce_fusion = (f32[1536]{0:T(1024)S(1)}, bf16[1024,1536]{1,0:T(8,128)(2,1)S(1)}) fusion(f32[1024,1536]{1,0:T(8,128)} %get-tuple-element.78, f32[1536]{0:T(1024)S(1)} %get-tuple-element.47, bf16[2,768,4608]{2,1,0:T(8,128)(2,1)S(1)} %bitcast.181, bf16[512,768]{1,0:T(8,128)(2,1)} %collective-permute-done.3, bf16[512,768]{1,0:T(8,128)(2,1)S(1)} %copy-done.12, ...), kind=kOutput, calls=%fused_computation.13 | convolution fusion | flops 2446588416 | bytes 13383681 | tf_op jit(solution)/shard_map/dot_general | solution.py:35
  208.9 3.4 convolution_convert_fusion.1
  212.2 5.2 %multiply_reduce_fusion = (f32[768]{0:T(1024)S(1)}, f32[1024]{0:T(1024)S(1)}, f32[1024]{0:T(1024)S(1)}, f32[768]{0:T(1024)S(1)}, f32[1024,768]{1,0:T(8,128)S(1)}) fusion(f32[1024,768]{1,0:T(8,128)S(1)} %get-tuple-element.75, f32[1024]{0:T(1024)S(1)} %add_rsqrt_fusion, f32[1024]{0:T(1024)S(1)} %broadcast_multiply_fusion.4, f32[768]{0:T(1024)S(1)} %copy-done.18, ...), kind=kOutput, calls=%fused_computation.56 | convolution fusion | flops 2423779840 | bytes 14968832 | tf_op jit(solution)/shard_map/dot_general | solution.py:39
  217.5 3.9 fusion.59
  225.4 4.4 %convolution_convert_fusion.2 = bf16[768,1536]{1,0:T(8,128)(2,1)S(1)} fusion(bf16[1024,1536]{1,0:T(8,128)(2,1)S(1)} %copy-done.29, bf16[512,768]{1,0:T(8,128)(2,1)} %collective-permute-done.3, bf16[512,768]{1,0:T(8,128)(2,1)S(1)} %copy-done.12, pred[]{:T(512)S(6)} %eq.7), kind=kOutput, calls=%fused_computation.41 | convolution fusion | flops 2424176640 | bytes 7077889 | tf_op jit(solution)/shard_map/dot_general | solution.py:43
  230.3 1.4 copy-done.27
  231.8 4.4 %convolution_convert_fusion = bf16[768,1536]{1,0:T(8,128)(2,1)S(1)} fusion(bf16[1024,1536]{1,0:T(8,128)(2,1)S(1)} %copy-done.27, bf16[512,768]{1,0:T(8,128)(2,1)} %collective-permute-done.3, bf16[512,768]{1,0:T(8,128)(2,1)S(1)} %copy-done.12, pred[]{:T(512)S(6)} %eq.7), kind=kOutput, calls=%fused_computation.39 | convolution fusion | flops 2424176640 | bytes 7077889 | tf_op jit(solution)/shard_map/dot_general | solution.py:43
  236.6 4.8 %pad_maximum_fusion = bf16[2,768,3456]{2,1,0:T(8,128)(2,1)} fusion(bf16[1,768,3456]{2,1,0:T(8,128)(2,1)S(1)} %maximum_bitcast_fusion.1, bf16[1,768,3456]{2,1,0:T(8,128)(2,1)S(1)} %maximum_bitcast_fusion), kind=kLoop, calls=%fused_computation | loop fusion | flops 5308416 | bytes 21233664 | tf_op jit(solution)/shard_map/stack | solution.py:382
  241.6 69.1 %attend_back.1 = (bf16[2,1024,1152]{2,1,0:T(8,128)(2,1)}, f32[3,64]{1,0:T(4,128)}) custom-call(bf16[1024,768]{1,0:T(8,128)(2,1)} %copy-done.10, bf16[2,768,4608]{2,1,0:T(8,128)(2,1)} %bitcast.172, f32[2,1024,1152]{2,1,0:T(8,128)} %get-tuple-element.31.p_ref, f32[1,64]{1,0:T(1,128)} %bitcast.203, f32[1,64]{1,0:T(1,128)} %bitcast.205, f32[1,64]{1,0:T(1,128)} %bitcast.207, ...), custom_call_target="tpu_custom_call" | custom-call | flops 4831838208 | bytes 14155776 | tf_op jit(solution)/shard_map/attend_back/pallas_call | solution.py:230
  310.7 4.1 fusion.27
  314.8 2.3 fusion.28
  317.5 1.5 dynamic-slice_bitcast_fusion
  320.7 4.0 fusion.29
  324.7 6.4 %fusion.23 = (f32[768]{0:T(1024)S(1)}, f32[1024]{0:T(1024)S(1)}, f32[1024]{0:T(1024)S(1)}, f32[768]{0:T(1024)S(1)}, f32[1024,768]{1,0:T(8,128)}) fusion(f32[1024]{0:T(1024)S(1)} %add_rsqrt_fusion.1, f32[1024]{0:T(1024)S(1)} %broadcast_multiply_fusion.5, bf16[512,768]{1,0:T(8,128)(2,1)S(1)} %copy-done.3, bf16[512,768]{1,0:T(8,128)(2,1)S(1)} %copy-done.9, ...), kind=kOutput, calls=%fused_computation.51 | convolution fusion | flops 1827664384 | bytes 12019713 | tf_op jit(solution)/shard_map/dot_general | solution.py:39
  331.1 1.5 collective-permute-start.6
  332.6 5.3 %fusion.22 = f32[1024,768]{1,0:T(8,128)S(1)} fusion(f32[1024,768]{1,0:T(8,128)} %copy-done, f32[1024,768]{1,0:T(8,128)} %get-tuple-element.81, f32[1024]{0:T(1024)S(1)} %broadcast_multiply_fusion, f32[1024]{0:T(1024)S(1)} %broadcast_multiply_fusion.1, f32[768]{0:T(1024)S(1)} %copy-done.17, f32[1024]{0:T(1024)S(1)} %add_rsqrt_fusion.1, ...), kind=kLoop, calls=%fused_computation.50 | loop fusion | flops 14155776 | bytes 11029505 | tf_op jit(solution)/shard_map/add | solution.py:432
  339.7 4.8 %fusion.37 = f32[1024,768]{1,0:T(8,128)S(1)} fusion(bf16[1024,1536]{1,0:T(8,128)(2,1)S(1)} %copy-done.30, bf16[2,768,4608]{2,1,0:T(8,128)(2,1)} %bitcast.175), kind=kOutput, calls=%fused_computation.78 | convolution fusion | flops 2415919104 | bytes 8650752 | tf_op jit(solution)/shard_map/dot_general | solution.py:39
  345.7 1.9 fusion.16
  348.3 4.3 %add_convert_fusion = bf16[1024,768]{1,0:T(8,128)(2,1)S(1)} fusion(f32[1024,768]{1,0:T(8,128)S(1)} %fusion.37, f32[1024,768]{1,0:T(8,128)S(1)} %get-tuple-element.75, f32[768]{0:T(1024)S(1)} %copy-done.26, bf16[1024,1536]{1,0:T(8,128)(2,1)S(1)} %copy-done.28, bf16[2,768,4608]{2,1,0:T(8,128)(2,1)} %bitcast.176), kind=kOutput, calls=%fused_computation.57 | convolution fusion | flops 2419064832 | bytes 13372416 | tf_op jit(solution)/shard_map/dot_general | solution.py:39
  353.8 3.6 collective-permute-done.9
  357.4 1.2 collective-permute-start.10
  358.6 1.3 constant_dynamic-slice_fusion.2
  359.9 1.5 collective-permute-start.4
  361.4 3.4 collective-permute-done.10
  365.5 20.1 %collective-permute-done.12 = bf16[8,48,1152]{2,1,0:T(8,128)(2,1)S(1)} collective-permute-done((bf16[8,48,1152]{2,1,0:T(8,128)(2,1)S(1)}, bf16[8,48,1152]{2,1,0:T(8,128)(2,1)S(1)}, u32[]{:S(2)}, u32[]{:S(2)}) %collective-permute-start.12) | collective-permute-done | bytes 884768 | tf_op jit(solution)/shard_map/ppermute | solution.py:418
  388.9 7.5 %collective-permute-done.13 = bf16[1,4,48,1152]{3,2,1,0:T(8,128)(2,1)S(1)} collective-permute-done((bf16[1,4,48,1152]{3,2,1,0:T(8,128)(2,1)}, bf16[1,4,48,1152]{3,2,1,0:T(8,128)(2,1)S(1)}, u32[]{:S(2)}, u32[]{:S(2)}) %collective-permute-start.13) | collective-permute-done | bytes 442400 | tf_op jit(solution)/shard_map/ppermute | solution.py:159
  397.7 1.2 bitcast_convert_fusion
  399.0 1.9 maximum_select_fusion
  400.9 2.9 collective-permute-done.14
  403.8 1.7 collective-permute-start.15
  405.5 2.9 maximum_select_fusion.3
  408.4 1.8 collective-permute-done.15
  413.5 1.6 slice.173
  (151 shorter events, 29.6 us)
Async XLA Ops:
  7.2 3.2 copy-start.14
  7.2 7.2 %copy-start.23 = (s32[2,512]{1,0:T(2,128)S(1)}, s32[2,512]{1,0:T(2,128)}, u32[]{:S(2)}) copy-start(s32[2,512]{1,0:T(2,128)} %param.19) | copy-start | bytes 12292
  7.2 7.3 %copy-start.20 = (f32[3,384]{1,0:T(4,128)S(1)}, f32[3,384]{1,0:T(4,128)}, u32[]{:S(2)}) copy-start(f32[3,384]{1,0:T(4,128)} %param.24) | copy-start | bytes 13828
  7.2 7.3 %copy-start.19 = (f32[1536]{0:T(1024)S(1)}, f32[1536]{0:T(1024)}, u32[]{:S(2)}) copy-start(f32[1536]{0:T(1024)} %param.33) | copy-start | bytes 18436
  7.2 119.0 %all-gather.2.cloned.1.call-start = ((), (), s32[]{:S(2)}) async-start(), calls=%async_computation.1 | async-start | bytes 14598144 | tf_op jit(solution)/shard_map/all_gather | solution.py:328
  10.3 400.8 %reduce-scatter.2.cloned.1.call-start = ((), (), s32[]{:S(2)}) async-start(), calls=%async_computation.2 | async-start | bytes 10948608 | tf_op jit(solution)/shard_map/reduce_scatter | solution.py:386
  11.4 28.7 %copy-start.1 = (bf16[512,768]{1,0:T(8,128)(2,1)}, bf16[512,768]{1,0:T(8,128)(2,1)S(1)}, u32[]{:S(2)}) copy-start(bf16[512,768]{1,0:T(8,128)(2,1)S(1)} %get-tuple-element.57) | copy-start | bytes 2359300
  11.4 27.4 %collective-permute-start = (bf16[512,768]{1,0:T(8,128)(2,1)}, bf16[512,768]{1,0:T(8,128)(2,1)S(1)}, u32[]{:S(2)}, u32[]{:S(2)}) collective-permute-start(bf16[512,768]{1,0:T(8,128)(2,1)} %get-tuple-element.56), channel_id=1, source_target_pairs={{0,1},{1,0},{2,3},{3,2},{4,5},{5,4},{6,7},{7,6},{8,9},{9,8},{10,11... | collective-permute-start | bytes 2359304 | tf_op jit(solution)/shard_map/ppermute | solution.py:311
  14.4 21.8 %collective-permute-start.2 = (s32[512]{0:T(512)S(1)}, s32[512]{0:T(512)S(1)}, u32[]{:S(2)}, u32[]{:S(2)}) collective-permute-start(s32[512]{0:T(512)S(1)} %bitcast.201), channel_id=1, source_target_pairs={{0,1},{1,0},{2,3},{3,2},{4,5},{5,4},{6,7},{7,6},{8,9},{9,8},{10,11... | collective-permute-start | bytes 6152 | tf_op jit(solution)/shard_map/ppermute | solution.py:311
  14.5 23.6 %collective-permute-start.1 = (f32[2688]{0:T(1024)S(1)}, f32[2688]{0:T(1024)S(1)}, u32[]{:S(2)}, u32[]{:S(2)}) collective-permute-start(f32[2688]{0:T(1024)S(1)} %constant_dynamic-update-slice_fusion), channel_id=1, source_target_pairs={{0,1},{1,0},{2,3},{3,2},{4,5},{5,4},{6,7},{7,6},{8,9},{9,8},{10,11... | collective-permute-start | bytes 32264 | tf_op jit(solution)/shard_map/ppermute | solution.py:340
  19.2 20.9 %copy-start.17 = (f32[768]{0:T(1024)S(1)}, f32[768]{0:T(1024)}, u32[]{:S(2)}) copy-start(f32[768]{0:T(1024)} %param.21) | copy-start | bytes 9220
  19.2 20.9 %copy-start.21 = (f32[768]{0:T(1024)S(1)}, f32[768]{0:T(1024)}, u32[]{:S(2)}) copy-start(f32[768]{0:T(1024)} %param.22) | copy-start | bytes 9220
  19.2 161.9 %collective-permute-start.3 = (bf16[512,768]{1,0:T(8,128)(2,1)}, bf16[512,768]{1,0:T(8,128)(2,1)}, u32[]{:S(2)}, u32[]{:S(2)}) collective-permute-start(bf16[512,768]{1,0:T(8,128)(2,1)} %get-tuple-element.55), channel_id=1, source_target_pairs={{0,1},{1,0},{2,3},{3,2},{4,5},{5,4},{6,7},{7,6},{8,9},{9,8},{10,11... | collective-permute-start | bytes 2359304 | tf_op jit(solution)/shard_map/ppermute | solution.py:311
  38.8 4.4 %copy-start.7 = (bf16[512,768]{1,0:T(8,128)(2,1)}, bf16[512,768]{1,0:T(8,128)(2,1)S(1)}, u32[]{:S(2)}) copy-start(bf16[512,768]{1,0:T(8,128)(2,1)S(1)} %collective-permute-done) | copy-start | bytes 2359300
  168.2 2.5 copy-start.2
  168.2 2.5 copy-start.8
  168.2 2.5 copy-start.16
  168.2 2.5 copy-start.25
  170.7 5.2 %copy-start.4 = (bf16[1536,4608]{1,0:T(8,128)(2,1)S(1)}, bf16[1536,4608]{1,0:T(8,128)(2,1)}, u32[]{:S(2)}) copy-start(bf16[1536,4608]{1,0:T(8,128)(2,1)} %all-gather.2.cloned.1.call-done) | copy-start | bytes 42467332
  173.3 1.5 copy-start.22
  175.9 5.2 %copy-start.12 = (bf16[512,768]{1,0:T(8,128)(2,1)S(1)}, bf16[512,768]{1,0:T(8,128)(2,1)}, u32[]{:S(2)}) copy-start(bf16[512,768]{1,0:T(8,128)(2,1)} %get-tuple-element.54) | copy-start | bytes 2359300
  221.4 1.7 copy-start
  221.6 2.0 copy-start.10
  223.5 1.9 copy-start.29
  229.9 1.9 copy-start.27
  241.6 69.1 %copy-start.15 = (bf16[1024,768]{1,0:T(8,128)(2,1)S(1)}, bf16[1024,768]{1,0:T(8,128)(2,1)}, u32[]{:S(2)}) copy-start(bf16[1024,768]{1,0:T(8,128)(2,1)} %fusion.18.x_ref) | copy-start | bytes 4718596
  310.7 4.2 copy-start.11
  317.5 2.5 copy-start.5
  317.5 1.7 copy-start.24
  319.0 26.7 %collective-permute-start.11 = (bf16[2,8,48,1152]{3,2,1,0:T(8,128)(2,1)}, bf16[2,8,48,1152]{3,2,1,0:T(8,128)(2,1)}, u32[]{:S(2)}, u32[]{:S(2)}) collective-permute-start(bf16[2,8,48,1152]{3,2,1,0:T(8,128)(2,1)} %dynamic-slice_bitcast_fusion), channel_id=1, source_target_pairs={{0,2},{2,0},{4,6},{6,4},{8,10},{10,8},{12,14},{14,12},{16,18},{18,... | collective-permute-start | bytes 5308424 | tf_op jit(solution)/shard_map/ppermute | solution.py:159
  320.6 4.0 copy-start.3
  320.6 4.0 copy-start.9
  331.1 8.5 %collective-permute-start.6 = (f32[10176]{0:T(1024)S(1)}, f32[10176]{0:T(1024)S(1)}, u32[]{:S(2)}, u32[]{:S(2)}) collective-permute-start(f32[10176]{0:T(1024)S(1)} %concatenate.94), channel_id=1, source_target_pairs={{0,1},{1,0},{2,3},{3,2},{4,5},{5,4},{6,7},{7,6},{8,9},{9,8},{10,11... | collective-permute-start | bytes 122120 | tf_op jit(solution)/shard_map/ppermute | solution.py:168
  332.6 7.1 %copy-start.30 = (bf16[1024,1536]{1,0:T(8,128)(2,1)S(1)}, bf16[1024,1536]{1,0:T(8,128)(2,1)}, u32[]{:S(2)}) copy-start(bf16[1024,1536]{1,0:T(8,128)(2,1)} %get-tuple-element.28) | copy-start | bytes 9437188
  338.9 58.8 %collective-permute-start.5 = (bf16[512,768]{1,0:T(8,128)(2,1)}, bf16[512,768]{1,0:T(8,128)(2,1)}, u32[]{:S(2)}, u32[]{:S(2)}) collective-permute-start(bf16[512,768]{1,0:T(8,128)(2,1)} %fusion.51), channel_id=1, source_target_pairs={{0,1},{1,0},{2,3},{3,2},{4,5},{5,4},{6,7},{7,6},{8,9},{9,8},{10,11... | collective-permute-start | bytes 2359304 | tf_op jit(solution)/shard_map/ppermute | solution.py:315
  339.6 6.0 %copy-start.6 = (bf16[2,768,1152]{2,1,0:T(8,128)(2,1)S(1)}, bf16[2,768,1152]{2,1,0:T(8,128)(2,1)}, u32[]{:S(2)}) copy-start(bf16[2,768,1152]{2,1,0:T(8,128)(2,1)} %copy-done.5) | copy-start | bytes 10616836
  339.7 4.9 %collective-permute-start.7 = (f32[10176]{0:T(1024)S(1)}, f32[10176]{0:T(1024)S(1)}, u32[]{:S(2)}, u32[]{:S(2)}) collective-permute-start(f32[10176]{0:T(1024)S(1)} %add.236), channel_id=1, source_target_pairs={{0,2},{2,0},{4,6},{6,4},{8,10},{10,8},{12,14},{14,12},{16,18},{18,... | collective-permute-start | bytes 122120 | tf_op jit(solution)/shard_map/ppermute | solution.py:168
  344.6 3.7 copy-start.26
  344.6 3.7 copy-start.28
  344.6 8.0 %collective-permute-start.8 = (f32[10176]{0:T(1024)S(1)}, f32[10176]{0:T(1024)S(1)}, u32[]{:S(2)}, u32[]{:S(2)}) collective-permute-start(f32[10176]{0:T(1024)S(1)} %add.237), channel_id=1, source_target_pairs={{0,4},{2,6},{4,0},{6,2},{8,12},{10,14},{12,8},{14,10},{16,20},{18,... | collective-permute-start | bytes 122120 | tf_op jit(solution)/shard_map/ppermute | solution.py:168
  347.7 37.9 %collective-permute-start.12 = (bf16[8,48,1152]{2,1,0:T(8,128)(2,1)S(1)}, bf16[8,48,1152]{2,1,0:T(8,128)(2,1)S(1)}, u32[]{:S(2)}, u32[]{:S(2)}) collective-permute-start(bf16[8,48,1152]{2,1,0:T(8,128)(2,1)S(1)} %dynamic-slice_bitcast_fusion.1), channel_id=1, source_target_pairs={{0,1},{1,0},{2,3},{3,2},{4,5},{5,4},{6,7},{7,6},{8,9},{9,8},{10,11... | collective-permute-start | bytes 2654216 | tf_op jit(solution)/shard_map/ppermute | solution.py:418
  352.7 4.7 %collective-permute-start.9 = (f32[10176]{0:T(1024)S(1)}, f32[10176]{0:T(1024)S(1)}, u32[]{:S(2)}, u32[]{:S(2)}) collective-permute-start(f32[10176]{0:T(1024)S(1)} %add.238), channel_id=1, source_target_pairs={{0,8},{2,10},{4,12},{6,14},{8,0},{10,2},{12,4},{14,6},{16,24},{18,... | collective-permute-start | bytes 122120 | tf_op jit(solution)/shard_map/ppermute | solution.py:168
  357.4 7.4 %collective-permute-start.10 = (f32[10176]{0:T(1024)S(1)}, f32[10176]{0:T(1024)S(1)}, u32[]{:S(2)}, u32[]{:S(2)}) collective-permute-start(f32[10176]{0:T(1024)S(1)} %add.239), channel_id=1, source_target_pairs={{0,16},{2,18},{4,20},{6,22},{8,24},{10,26},{12,28},{14,30},{16,0},... | collective-permute-start | bytes 122120 | tf_op jit(solution)/shard_map/ppermute | solution.py:168
  359.9 45.6 %collective-permute-start.4 = (bf16[512,768]{1,0:T(8,128)(2,1)}, bf16[512,768]{1,0:T(8,128)(2,1)}, u32[]{:S(2)}, u32[]{:S(2)}) collective-permute-start(bf16[512,768]{1,0:T(8,128)(2,1)} %get-tuple-element.53), channel_id=1, source_target_pairs={{0,1},{1,0},{2,3},{3,2},{4,5},{5,4},{6,7},{7,6},{8,9},{9,8},{10,11... | collective-permute-start | bytes 2359304 | tf_op jit(solution)/shard_map/ppermute | solution.py:315
  386.6 9.7 %collective-permute-start.13 = (bf16[1,4,48,1152]{3,2,1,0:T(8,128)(2,1)}, bf16[1,4,48,1152]{3,2,1,0:T(8,128)(2,1)S(1)}, u32[]{:S(2)}, u32[]{:S(2)}) collective-permute-start(bf16[1,4,48,1152]{3,2,1,0:T(8,128)(2,1)} %dynamic-slice_bitcast_fusion.7), channel_id=1, source_target_pairs={{0,4},{2,6},{4,0},{6,2},{8,12},{10,14},{12,8},{14,10},{16,20},{18,... | collective-permute-start | bytes 1327112 | tf_op jit(solution)/shard_map/ppermute | solution.py:159
  396.5 7.2 %collective-permute-start.14 = (bf16[1,2,48,1152]{3,2,1,0:T(8,128)(2,1)S(1)}, bf16[1,2,48,1152]{3,2,1,0:T(8,128)(2,1)S(1)}, u32[]{:S(2)}, u32[]{:S(2)}) collective-permute-start(bf16[1,2,48,1152]{3,2,1,0:T(8,128)(2,1)S(1)} %dynamic-slice_bitcast_fusion.8), channel_id=1, source_target_pairs={{0,8},{2,10},{4,12},{6,14},{8,0},{10,2},{12,4},{14,6},{16,24},{18,... | collective-permute-start | bytes 663560 | tf_op jit(solution)/shard_map/ppermute | solution.py:159
  399.0 6.5 %copy-start.13 = (bf16[1,512,768]{2,1,0:T(8,128)(2,1)S(1)}, bf16[1,512,768]{2,1,0:T(8,128)(2,1)}, u32[]{:S(2)}) copy-start(bf16[1,512,768]{2,1,0:T(8,128)(2,1)} %get-tuple-element.52) | copy-start | bytes 2359300
  403.8 6.3 %collective-permute-start.15 = (bf16[1,1,48,1152]{3,2,1,0:T(8,128)(2,1)S(1)}, bf16[1,1,48,1152]{3,2,1,0:T(8,128)(2,1)S(1)}, u32[]{:S(2)}, u32[]{:S(2)}) collective-permute-start(bf16[1,1,48,1152]{3,2,1,0:T(8,128)(2,1)S(1)} %constant_dynamic-slice_fusion), channel_id=1, source_target_pairs={{0,16},{2,18},{4,20},{6,22},{8,24},{10,26},{12,28},{14,30},{16,0},... | collective-permute-start | bytes 331784 | tf_op jit(solution)/shard_map/ppermute | solution.py:159
  (1 other events, 1.4 us)
Sparse Core Ops, SparseCore 0:
  11.5 114.6 all-gather.1
  241.6 145.5 reduce-scatter.1

commit v4 on v3

--- a/solution.py
+++ b/solution.py
@@ -47,24 +47,37 @@
     return max(0, block - REACH), min(count, block + REACH + 1)
 
 
+def head_means(values, table):
+    high = values.astype(BF)
+    low = (values - high.astype(F32)).astype(BF)
+    return mm(high, table) + mm(low, table)
+
+
+def head_norm_parts(values, table):
+    centred = values - head_means(values, table)
+    scaled = lax.rsqrt(head_means(centred * centred, table) + EPSILON)
+    return (centred * scaled, scaled)
+
+
 def attend_kernel(
-    x_ref, w_ref, b_ref, qg_ref, qb_ref, kg_ref, idc_ref, idr_ref, p_ref, mixed_ref, *, depth
+    x_ref, w_ref, b_ref, table_ref, gain_ref, shift_ref, idc_ref, idr_ref, p_ref, mixed_ref,
+    *, depth
 ):
     length = x_ref.shape[0]
     lanes = mixed_ref.shape[1]
     count = length // BLOCK
-    scale = depth ** (-0.5)
     project = mm(x_ref[...], w_ref[0]) + b_ref[0]
     p_ref[0] = project
+    unit, _ = head_norm_parts(project[:, : 2 * lanes], table_ref[...])
+    normed = (unit * gain_ref[...] + shift_ref[...]).astype(BF)
+    queries = normed[:, :lanes] * jnp.asarray(depth ** (-0.5), BF)
+    values = project[:, 2 * lanes :].astype(BF)
     heads = []
     for head in range(lanes // depth):
-        part = [
-            project[:, i * lanes + head * depth : i * lanes + (head + 1) * depth] for i in range(3)
-        ]
-        query = (norm_parts(part[0])[0] * qg_ref[...] + qb_ref[...]).astype(BF)
-        query = query * jnp.asarray(scale, BF)
-        key = (norm_parts(part[1])[0] * kg_ref[...]).astype(BF)
-        value = part[2].astype(BF)
+        columns = slice(head * depth, (head + 1) * depth)
+        query = queries[:, columns]
+        key = normed[:, lanes + head * depth : lanes + (head + 1) * depth]
+        value = values[:, columns]
         value = jnp.concatenate([value, jnp.ones_like(value)], axis=1)
         rows = []
         for block in range(count):
@@ -81,27 +94,25 @@
 
 
 def attend_back_kernel(
-    g_ref, w_ref, p_ref, qg_ref, qb_ref, kg_ref, idc_ref, idr_ref, gp_ref, sums_ref, *, depth
+    g_ref, w_ref, p_ref, table_ref, gain_ref, shift_ref, idc_ref, idr_ref, gp_ref, sums_ref,
+    *, depth
 ):
     length = g_ref.shape[0]
     lanes = w_ref.shape[2]
     count = length // BLOCK
     scale = depth ** (-0.5)
     grad_mixed = mm(g_ref[...], w_ref[0]).astype(BF)
-    project = p_ref[0]
-    sums = [jnp.zeros((1, depth), F32) for _ in range(3)]
-    columns = [[], [], []]
+    unit, scaled = head_norm_parts(p_ref[0, :, : 2 * lanes], table_ref[...])
+    normed = (unit * gain_ref[...] + shift_ref[...]).astype(BF)
+    queries = normed[:, :lanes] * jnp.asarray(scale, BF)
+    values = p_ref[0, :, 2 * lanes :].astype(BF)
+    grad_queries, grad_keys, grad_values = [], [], []
     for head in range(lanes // depth):
-        part = [
-            project[:, i * lanes + head * depth : i * lanes + (head + 1) * depth] for i in range(3)
-        ]
-        query_unit, query_scaled = norm_parts(part[0])
-        key_unit, key_scaled = norm_parts(part[1])
-        query = (query_unit * qg_ref[...] + qb_ref[...]).astype(BF)
-        query = query * jnp.asarray(scale, BF)
-        key = (key_unit * kg_ref[...]).astype(BF)
-        value = part[2].astype(BF)
-        grad = grad_mixed[:, head * depth : (head + 1) * depth]
+        columns = slice(head * depth, (head + 1) * depth)
+        query = queries[:, columns]
+        key = normed[:, lanes + head * depth : lanes + (head + 1) * depth]
+        value = values[:, columns]
+        grad = grad_mixed[:, columns]
         grad_key = [None] * count
         grad_value = [None] * count
         grad_query = []
@@ -125,24 +136,31 @@
                 grad_value[i] = (
                     to_value[piece] if grad_value[i] is None else grad_value[i] + to_value[piece]
                 )
-        grad_query = jnp.concatenate(grad_query, axis=0)
-        grad_key = jnp.concatenate(grad_key, axis=0)
-        grad_value = jnp.concatenate(grad_value, axis=0)
-        sums[0] += jnp.sum(grad_query * query_unit, axis=0, keepdims=True)
-        sums[1] += jnp.sum(grad_query, axis=0, keepdims=True)
-        sums[2] += jnp.sum(grad_key * key_unit, axis=0, keepdims=True)
-        columns[0].append(norm_back(grad_query, query_unit, query_scaled, qg_ref[...]))
-        columns[1].append(norm_back(grad_key, key_unit, key_scaled, kg_ref[...]))
-        columns[2].append(grad_value)
-    for i in range(3):
-        gp_ref[0, :, i * lanes : (i + 1) * lanes] = jnp.concatenate(columns[i], axis=1).astype(BF)
+        grad_queries.append(jnp.concatenate(grad_query, axis=0))
+        grad_keys.append(jnp.concatenate(grad_key, axis=0))
+        grad_values.append(jnp.concatenate(grad_value, axis=0))
+    grads = jnp.concatenate(grad_queries + grad_keys, axis=1)
+    grad_unit = grads * gain_ref[...]
+    first = head_means(grad_unit, table_ref[...])
+    second = head_means(grad_unit * unit, table_ref[...])
+    gp_ref[0, :, : 2 * lanes] = (scaled * (grad_unit - first - unit * second)).astype(BF)
+    gp_ref[0, :, 2 * lanes :] = jnp.concatenate(grad_values, axis=1).astype(BF)
 
     @pl.when(pl.program_id(0) == 0)
     def _():
         sums_ref[...] = jnp.zeros_like(sums_ref)
 
-    for i in range(3):
-        sums_ref[i : i + 1, :] += sums[i]
+    sums_ref[0:1, :] += jnp.sum(grads * unit, axis=0, keepdims=True)
+    sums_ref[1:2, :] += jnp.sum(grads, axis=0, keepdims=True)
+
+
+def head_operands(query_gain, query_bias, key_gain):
+    head = jnp.arange(4 * query_gain.shape[0]) // query_gain.shape[0]
+    table = jnp.where(head[:, None] == head[None], 1.0 / query_gain.shape[0], 0.0).astype(BF)
+    gain = jnp.concatenate([query_gain, query_gain, key_gain, key_gain])[None]
+    none = jnp.zeros_like(query_bias)
+    shift = jnp.concatenate([query_bias, query_bias, none, none])[None]
+    return table, gain, shift
 
 
 def add_halves(own, other):
@@ -159,15 +177,9 @@
     return add_halves(own, lax.ppermute(other, "fsdp", [(i, i ^ step) for i in range(size)]))
 
 
-def sum_by_pairs(vector, axes):
-    for axis in axes:
-        size = lax.axis_size(axis)
-        assert size & (size - 1) == 0
-        step = 1
-        while step < size:
-            vector = vector + lax.ppermute(vector, axis, [(i, i ^ step) for i in range(size)])
-            step *= 2
-    return vector
+def add_over_fsdp(vector, step):
+    size = lax.axis_size("fsdp")
+    return vector + lax.ppermute(vector, "fsdp", [(i, i ^ step) for i in range(size)])
 
 
 def attend(normed, weight, bias, query_gain, query_bias, key_gain, ids, local_width):
@@ -184,9 +196,9 @@
             whole(length, width),
             pl.BlockSpec((1, width, 3 * lanes), lambda i: (i // per, 0, i % per)),
             pl.BlockSpec((1, 1, 3 * lanes), lambda i: (i // per, 0, i % per)),
-            whole(1, depth),
-            whole(1, depth),
-            whole(1, depth),
+            whole(2 * lanes, 2 * lanes),
+            whole(1, 2 * lanes),
+            whole(1, 2 * lanes),
             whole(length, 1),
             whole(1, length),
         ],
@@ -209,9 +221,7 @@
         normed,
         weight,
         bias,
-        query_gain[None],
-        query_bias[None],
-        key_gain[None],
+        *head_operands(query_gain, query_bias, key_gain),
         ids[:, None],
         ids[None],
     )
@@ -234,19 +244,19 @@
             whole(length, width),
             pl.BlockSpec((1, width, lanes), lambda i: (i // per, 0, first + i % per)),
             pl.BlockSpec((1, length, 3 * lanes), lambda i: (i // per, 0, i % per)),
-            whole(1, depth),
-            whole(1, depth),
-            whole(1, depth),
+            whole(2 * lanes, 2 * lanes),
+            whole(1, 2 * lanes),
+            whole(1, 2 * lanes),
             whole(length, 1),
             whole(1, length),
         ],
         out_specs=[
             pl.BlockSpec((1, length, 3 * lanes), lambda i: (i // per, 0, i % per)),
-            whole(3, depth),
+            whole(2, 2 * lanes),
         ],
         out_shape=[
             jax.ShapeDtypeStruct((tp, length, 3 * local_width), BF),
-            jax.ShapeDtypeStruct((3, depth), F32),
+            jax.ShapeDtypeStruct((2, 2 * lanes), F32),
         ],
         compiler_params=pltpu.CompilerParams(vmem_limit_bytes=56 * 2**20),
         cost_estimate=pl.CostEstimate(
@@ -259,9 +269,7 @@
         grad_rows,
         weight,
         project,
-        query_gain[None],
-        query_bias[None],
-        key_gain[None],
+        *head_operands(query_gain, query_bias, key_gain),
         ids[:, None],
         ids[None],
     )
@@ -295,7 +303,8 @@
     shard = qkv_weight.shape[0]
     local_width = qkv_weight.shape[2]
     local_hidden = up_weight.shape[1]
-    lanes = 2 * query_gain.shape[0]
+    depth = query_gain.shape[0]
+    lanes = 2 * depth
     per = local_width // lanes
     swap = [(0, 1), (1, 0)]
 
@@ -412,32 +421,18 @@
         sums_qkv.append(jnp.sum(grad_project[i].astype(F32), axis=0))
     early = jnp.stack(terms_qkv)
     early, grad_project = lax.optimization_barrier((early, grad_project))
-    early = early.reshape(tp, -1, shard, edge_out)
-    early = halve_over_fsdp(early, 1)
-    early = add_halves(
-        pick(early, me), lax.ppermute(pick(early, 1 - me), "tp", swap)
-    )[None]
-    step = 2
-    while step < lax.axis_size("fsdp"):
-        early = halve_over_fsdp(early, step)
-        step *= 2
-    early = early.reshape(shard, edge_out).astype(F32)
+    early = halve_over_fsdp(early.reshape(tp, -1, shard, edge_out), 1)
     for i in range(tp):
         grad_normed1 = grad_normed1 + mm_nt(grad_project[i], qkv[i])
-    qkv_weight_grad = (
-        early.reshape(shard, per, 3, lanes)
-        .transpose(0, 2, 1, 3)
-        .reshape(qkv_weight.shape)
-    )
     input_grad = grad_resid + norm_back(grad_normed1, unit_one, scaled_one, norm1_gain)
     input_grad = from_sequence(input_grad, BF)
 
     vectors = [
         jnp.sum(grad_normed1 * unit_one, axis=0),
         jnp.sum(grad_normed1, axis=0),
-        head_sums[0],
-        head_sums[1],
-        head_sums[2],
+        head_sums[0, :depth] + head_sums[0, depth : 2 * depth],
+        head_sums[1, :depth] + head_sums[1, depth : 2 * depth],
+        head_sums[0, 2 * depth : 3 * depth] + head_sums[0, 3 * depth :],
         jnp.sum(grad_resid, axis=0),
         jnp.sum(grad_normed2 * unit_two, axis=0),
         jnp.sum(grad_normed2, axis=0),
@@ -445,7 +440,23 @@
         *sums_qkv,
         *sums_up,
     ]
-    summed = sum_by_pairs(jnp.concatenate(vectors), everyone)
+    summed, early = lax.optimization_barrier((jnp.concatenate(vectors), early))
+    received = lax.ppermute(pick(early, 1 - me), "tp", swap)
+    summed = summed + lax.ppermute(summed, "tp", swap)
+    early = add_halves(pick(early, me), received)[None]
+    step = 1
+    while step < lax.axis_size("fsdp"):
+        summed, early = lax.optimization_barrier((summed, early))
+        if 2 * step < lax.axis_size("fsdp"):
+            early = halve_over_fsdp(early, 2 * step)
+        summed = add_over_fsdp(summed, step)
+        step *= 2
+    early = early.reshape(shard, edge_out).astype(F32)
+    qkv_weight_grad = (
+        early.reshape(shard, per, 3, lanes)
+        .transpose(0, 2, 1, 3)
+        .reshape(qkv_weight.shape)
+    )
     pieces, start = [], 0
     for vector in vectors:
         pieces.append(summed[start : start + vector.shape[0]])

time: 426 us -> 410 us (0.962)
  Pallas kernels: 111 us -> 78.4 us
  waiting for transfers between devices: 139 us -> 158 us
    ppermute x6, waiting for transfers between devices: 27 us -> 48.6 us  [the longest x1 40.4 us: on_device(): summed = summed + lax.ppermute(summed, 'tp', swap)]
    pallas_call x1, Pallas kernels: 69.1 us -> 52.5 us  [attend_back(): pl.pallas_call(partial(attend_back_kernel, depth=depth), grid=(tp * per,)...]
    pallas_call x1, Pallas kernels: 41.9 us -> 25.9 us  [attend(): pl.pallas_call(partial(attend_kernel, depth=depth), grid=(tp * per,), in_...]
  transfers between devices with their start and end apart: 18 -> 18, of which waited for: 8 -> 9; matrix products, arithmetic and copies ran while one was open for 17% -> 17% of each run, Pallas kernels for 26% -> 19%
where the time goes in v4:
time: 410 us; the launch traced here: 406 us
  waiting for transfers between devices  158 us (39%)
  matrix products  83.9 us (20%)
  Pallas kernels  78.4 us (19%)
  other arithmetic  34.4 us (8%)
  local copies, waits for them, and re-layouts  19.5 us (5%)
  starting transfers between devices  17.4 us (4%)
  between operations  15.2 us (4%)
    all_gather x1, waiting for transfers between devices, on_device(): lax.all_gather(packed, everyone, axis=0, tiled=True).reshape(tp, width, -1)  83 us
    pallas_call x1, Pallas kernels, attend_back(): pl.pallas_call(partial(attend_back_kernel, depth=depth), grid=(tp * per,)...  52.5 us
    ppermute x1, waiting for transfers between devices, on_device(): summed = summed + lax.ppermute(summed, 'tp', swap)  40.4 us
    dot_general x8, matrix products, mm_nt(): lax.dot_general(a, b, (((1,), (1,)), ((), ())), preferred_element_type=F32)  33.4 us
    dot_general x4, matrix products, mm(): return jnp.dot(a, b, preferred_element_type=F32)  26.9 us
    pallas_call x1, Pallas kernels, attend(): pl.pallas_call(partial(attend_kernel, depth=depth), grid=(tp * per,), in_...  25.9 us
    dot_general x8, matrix products, mm_tn(): lax.dot_general(a, b, (((0,), (0,)), ((), ())), preferred_element_type=F32)  23.6 us
    ppermute x3, waiting for transfers between devices, to_sequence(): lax.ppermute(pick(array, 1 - me), 'tp', swap)  14.9 us
  transfers between devices with their start and end apart: 18, of which 9 were waited for; matrix products, arithmetic and copies ran while one was open for 17% of the time, Pallas kernels for 19%

profile of v4, /device:TPU:0, one launch (start us, length us, event | category | flops | bytes accessed | tf_op | source)
XLA Modules:
  0.0 406.3 jit_solution(1332144176765136788)
XLA Ops:
  8.5 1.8 pad_maximum_fusion.2
  11.4 3.0 collective-permute-start
  14.6 2.0 collective-permute-start.1
  16.6 2.6 dynamic-slice_bitcast_fusion.4
  21.4 14.9 %collective-permute-done.2 = s32[512]{0:T(512)S(1)} collective-permute-done((s32[512]{0:T(512)S(1)}, s32[512]{0:T(512)S(1)}, u32[]{:S(2)}, u32[]{:S(2)}) %collective-permute-start.2) | collective-permute-done | bytes 2080 | tf_op jit(solution)/shard_map/ppermute | solution.py:320
  40.2 3.1 fusion.18.x_ref
  43.2 83.0 %all-gather.2.cloned.1.call-done = bf16[1536,4608]{1,0:T(8,128)(2,1)} async-done(((bf16[48,4608]{1,0:T(8,128)(2,1)}), bf16[1536,4608]{1,0:T(8,128)(2,1)}) %all-gather.2.cloned.1.call-update) | async-done | bytes 14155792 | tf_op jit(solution)/shard_map/all_gather | solution.py:337
  126.3 25.9 %attend.1 = (f32[2,1024,1152]{2,1,0:T(8,128)}, bf16[1024,768]{1,0:T(8,128)(2,1)}) custom-call(bf16[1024,768]{1,0:T(8,128)(2,1)} %fusion.18.x_ref, bf16[2,768,4608]{2,1,0:T(8,128)(2,1)} %bitcast.170, f32[2,1,1152]{2,1,0:T(1,128)} %broadcast_in_dim.24.b_ref, bf16[256,256]{1,0:T(8,128)(2,1)} %select_convert_fusion.table_ref, f32[1,256]{1,0:T(1,128)} %bitcast.205, ...), custom_call_target="tpu_custom_call" | custom-call | flops 3623878656 | bytes 12582912 | tf_op jit(solution)/shard_map/attend/pallas_call | solution.py:192
  152.2 2.4 fusion.56
  154.7 2.6 fusion.62
  159.9 5.4 %multiply_convert_fusion.2 = (bf16[1024,1536]{1,0:T(8,128)(2,1)}, f32[1024,1536]{1,0:T(8,128)}) fusion(f32[1536]{0:T(1024)S(1)} %get-tuple-element.68, bf16[1024,768]{1,0:T(8,128)(2,1)S(1)} %add_convert_fusion.1, bf16[2,768,4608]{2,1,0:T(8,128)(2,1)S(1)} %bitcast.178), kind=kOutput, calls=%fused_computation.18 | convolution fusion | flops 2425356288 | bytes 13377536 | tf_op jit(solution)/shard_map/dot_general | solution.py:35
  165.4 7.8 %convert_reduce_fusion.1 = (f32[1536]{0:T(1024)S(1)}, bf16[1024,1536]{1,0:T(8,128)(2,1)S(1)}) fusion(f32[1024,1536]{1,0:T(8,128)} %get-tuple-element.100, f32[1536]{0:T(1024)S(1)} %get-tuple-element.68, bf16[2,768,4608]{2,1,0:T(8,128)(2,1)S(1)} %bitcast.179, bf16[512,768]{1,0:T(8,128)(2,1)} %collective-permute-done.3, bf16[512,768]{1,0:T(8,128)(2,1)S(1)} %copy-done.14, ...), kind=kOutput, calls=%fused_computation.14 | convolution fusion | flops 2446588416 | bytes 13383681 | tf_op jit(solution)/shard_map/dot_general | solution.py:35
  173.2 4.3 %fusion.38 = f32[1024,768]{1,0:T(8,128)} fusion(bf16[1024,1536]{1,0:T(8,128)(2,1)S(1)} %get-tuple-element.103, bf16[2,768,4608]{2,1,0:T(8,128)(2,1)S(1)} %bitcast.180), kind=kOutput, calls=%fused_computation.79 | convolution fusion | flops 2415919104 | bytes 8650752 | tf_op jit(solution)/shard_map/dot_general | solution.py:39
  177.5 3.2 convolution_convert_fusion.3
  180.6 5.9 %multiply_convert_fusion = (bf16[1024,1536]{1,0:T(8,128)(2,1)}, f32[1024,1536]{1,0:T(8,128)}) fusion(f32[1536]{0:T(1024)S(1)} %get-tuple-element.67, bf16[1024,768]{1,0:T(8,128)(2,1)S(1)} %add_convert_fusion.1, bf16[2,768,4608]{2,1,0:T(8,128)(2,1)S(1)} %bitcast.181), kind=kOutput, calls=%fused_computation.15 | convolution fusion | flops 2425356288 | bytes 13377536 | tf_op jit(solution)/shard_map/dot_general | solution.py:35
  186.5 7.8 %convert_reduce_fusion = (f32[1536]{0:T(1024)S(1)}, bf16[1024,1536]{1,0:T(8,128)(2,1)S(1)}) fusion(f32[1024,1536]{1,0:T(8,128)} %get-tuple-element.98, f32[1536]{0:T(1024)S(1)} %get-tuple-element.67, bf16[2,768,4608]{2,1,0:T(8,128)(2,1)S(1)} %bitcast.182, bf16[512,768]{1,0:T(8,128)(2,1)} %collective-permute-done.3, bf16[512,768]{1,0:T(8,128)(2,1)S(1)} %copy-done.14, ...), kind=kOutput, calls=%fused_computation.13 | convolution fusion | flops 2446588416 | bytes 13383681 | tf_op jit(solution)/shard_map/dot_general | solution.py:35
  194.3 3.0 convolution_convert_fusion.1
  197.3 5.2 %multiply_reduce_fusion = (f32[768]{0:T(1024)S(1)}, f32[1024]{0:T(1024)S(1)}, f32[1024]{0:T(1024)S(1)}, f32[768]{0:T(1024)S(1)}, f32[1024,768]{1,0:T(8,128)S(1)}) fusion(f32[1024,768]{1,0:T(8,128)S(1)} %get-tuple-element.95, f32[1024]{0:T(1024)S(1)} %add_rsqrt_fusion, f32[1024]{0:T(1024)S(1)} %broadcast_multiply_fusion.4, f32[768]{0:T(1024)S(1)} %copy-done.19, ...), kind=kOutput, calls=%fused_computation.56 | convolution fusion | flops 2423779840 | bytes 14968832 | tf_op jit(solution)/shard_map/dot_general | solution.py:39
  202.5 3.9 fusion.59
  210.5 4.8 %convolution_convert_fusion.2 = bf16[768,1536]{1,0:T(8,128)(2,1)S(1)} fusion(bf16[1024,1536]{1,0:T(8,128)(2,1)S(1)} %copy-done.33, bf16[512,768]{1,0:T(8,128)(2,1)} %collective-permute-done.3, bf16[512,768]{1,0:T(8,128)(2,1)S(1)} %copy-done.14, pred[]{:T(512)S(6)} %eq.18), kind=kOutput, calls=%fused_computation.41 | convolution fusion | flops 2424176640 | bytes 7077889 | tf_op jit(solution)/shard_map/dot_general | solution.py:43
  215.7 1.4 copy-done.31
  217.1 4.4 %convolution_convert_fusion = bf16[768,1536]{1,0:T(8,128)(2,1)S(1)} fusion(bf16[1024,1536]{1,0:T(8,128)(2,1)S(1)} %copy-done.31, bf16[512,768]{1,0:T(8,128)(2,1)} %collective-permute-done.3, bf16[512,768]{1,0:T(8,128)(2,1)S(1)} %copy-done.14, pred[]{:T(512)S(6)} %eq.18), kind=kOutput, calls=%fused_computation.39 | convolution fusion | flops 2424176640 | bytes 7077889 | tf_op jit(solution)/shard_map/dot_general | solution.py:43
  221.9 4.8 %pad_maximum_fusion = bf16[2,768,3456]{2,1,0:T(8,128)(2,1)} fusion(bf16[1,768,3456]{2,1,0:T(8,128)(2,1)S(1)} %maximum_bitcast_fusion.1, bf16[1,768,3456]{2,1,0:T(8,128)(2,1)S(1)} %maximum_bitcast_fusion), kind=kLoop, calls=%fused_computation | loop fusion | flops 5308416 | bytes 21233664 | tf_op jit(solution)/shard_map/stack | solution.py:391
  226.9 52.5 %attend_back.1 = (bf16[2,1024,1152]{2,1,0:T(8,128)(2,1)}, f32[2,256]{1,0:T(2,128)}) custom-call(bf16[1024,768]{1,0:T(8,128)(2,1)} %copy-done.12, bf16[2,768,4608]{2,1,0:T(8,128)(2,1)} %bitcast.173, f32[2,1024,1152]{2,1,0:T(8,128)} %get-tuple-element.41.p_ref, bf16[256,256]{1,0:T(8,128)(2,1)} %select_convert_fusion.table_ref, f32[1,256]{1,0:T(1,128)} %bitcast.206, ...), custom_call_target="tpu_custom_call" | custom-call | flops 4831838208 | bytes 14155776 | tf_op jit(solution)/shard_map/attend_back/pallas_call | solution.py:240
  279.4 4.1 fusion.27
  283.5 2.3 fusion.28
  286.1 1.5 dynamic-slice_bitcast_fusion
  289.2 3.9 fusion.29
  293.1 6.2 %fusion.23 = (f32[768]{0:T(1024)S(1)}, f32[1024]{0:T(1024)S(1)}, f32[1024]{0:T(1024)S(1)}, f32[768]{0:T(1024)S(1)}, f32[1024,768]{1,0:T(8,128)}) fusion(f32[1024]{0:T(1024)S(1)} %add_rsqrt_fusion.1, f32[1024]{0:T(1024)S(1)} %broadcast_multiply_fusion.5, bf16[512,768]{1,0:T(8,128)(2,1)S(1)} %copy-done.4, bf16[512,768]{1,0:T(8,128)(2,1)S(1)} %copy-done.10, ...), kind=kOutput, calls=%fused_computation.51 | convolution fusion | flops 1827664384 | bytes 12019713 | tf_op jit(solution)/shard_map/dot_general | solution.py:39
  299.5 2.6 fusion.16
  302.2 1.5 collective-permute-start.8
  303.7 4.7 %fusion.22 = f32[1024,768]{1,0:T(8,128)S(1)} fusion(f32[1024,768]{1,0:T(8,128)S(1)} %copy-done.1, f32[1024,768]{1,0:T(8,128)} %get-tuple-element.101, f32[1024]{0:T(1024)S(1)} %broadcast_multiply_fusion, f32[1024]{0:T(1024)S(1)} %broadcast_multiply_fusion.1, f32[768]{0:T(1024)S(1)} %copy-done.18, f32[1024]{0:T(1024)S(1)} %add_rsqrt_fusion.1, ...), kind=kLoop, calls=%fused_computation.50 | loop fusion | flops 14155776 | bytes 11029505 | tf_op jit(solution)/shard_map/add | solution.py:427
  308.9 1.6 collective-permute-start.7
  310.5 4.4 %fusion.37 = f32[1024,768]{1,0:T(8,128)S(1)} fusion(bf16[1024,1536]{1,0:T(8,128)(2,1)S(1)} %copy-done.34, bf16[2,768,4608]{2,1,0:T(8,128)(2,1)} %bitcast.176), kind=kOutput, calls=%fused_computation.78 | convolution fusion | flops 2415919104 | bytes 8650752 | tf_op jit(solution)/shard_map/dot_general | solution.py:39
  314.9 40.4 %collective-permute-done.7 = f32[10176]{0:T(1024)S(1)} collective-permute-done((f32[10176]{0:T(1024)S(1)}, f32[10176]{0:T(1024)S(1)}, u32[]{:S(2)}, u32[]{:S(2)}) %collective-permute-start.7) | collective-permute-done | bytes 40736 | tf_op jit(solution)/shard_map/ppermute | solution.py:445
  355.6 1.6 collective-permute-start.10
  357.1 4.4 %add_convert_fusion = bf16[1024,768]{1,0:T(8,128)(2,1)S(1)} fusion(f32[1024,768]{1,0:T(8,128)S(1)} %fusion.37, f32[1024,768]{1,0:T(8,128)S(1)} %get-tuple-element.95, f32[768]{0:T(1024)S(1)} %copy-done.30, bf16[1024,1536]{1,0:T(8,128)(2,1)S(1)} %copy-done.32, bf16[2,768,4608]{2,1,0:T(8,128)(2,1)} %bitcast.177), kind=kOutput, calls=%fused_computation.57 | convolution fusion | flops 2419064832 | bytes 13372416 | tf_op jit(solution)/shard_map/dot_general | solution.py:39
  363.0 6.9 %collective-permute-done.10 = bf16[1,4,48,1152]{3,2,1,0:T(8,128)(2,1)S(1)} collective-permute-done((bf16[1,4,48,1152]{3,2,1,0:T(8,128)(2,1)S(1)}, bf16[1,4,48,1152]{3,2,1,0:T(8,128)(2,1)S(1)}, u32[]{:S(2)}, u32[]{:S(2)}) %collective-permute-start.10) | collective-permute-done | bytes 442400 | tf_op jit(solution)/shard_map/ppermute | solution.py:177
  370.0 1.3 collective-permute-start.12
  371.4 1.5 collective-permute-start.11
  373.0 2.4 collective-permute-done.11
  375.4 4.2 %collective-permute-done.12 = bf16[1,2,48,1152]{3,2,1,0:T(8,128)(2,1)S(1)} collective-permute-done((bf16[1,2,48,1152]{3,2,1,0:T(8,128)(2,1)S(1)}, bf16[1,2,48,1152]{3,2,1,0:T(8,128)(2,1)S(1)}, u32[]{:S(2)}, u32[]{:S(2)}) %collective-permute-start.12) | collective-permute-done | bytes 221216 | tf_op jit(solution)/shard_map/ppermute | solution.py:177
  379.7 2.3 collective-permute-start.14
  382.8 1.9 maximum_select_fusion
  384.7 2.9 collective-permute-done.13
  387.8 1.4 maximum_select_fusion.3
  390.1 2.5 collective-permute-done.15
  397.6 1.6 slice.185
  (164 shorter events, 27.8 us)
Async XLA Ops:
  7.2 3.2 copy-start.15
  7.2 7.2 %copy-start.25 = (s32[2,512]{1,0:T(2,128)S(1)}, s32[2,512]{1,0:T(2,128)}, u32[]{:S(2)}) copy-start(s32[2,512]{1,0:T(2,128)} %param.19) | copy-start | bytes 12292
  7.2 7.3 %copy-start.21 = (f32[3,384]{1,0:T(4,128)S(1)}, f32[3,384]{1,0:T(4,128)}, u32[]{:S(2)}) copy-start(f32[3,384]{1,0:T(4,128)} %param.24) | copy-start | bytes 13828
  7.2 7.3 %copy-start.20 = (f32[1536]{0:T(1024)S(1)}, f32[1536]{0:T(1024)}, u32[]{:S(2)}) copy-start(f32[1536]{0:T(1024)} %param.33) | copy-start | bytes 18436
  7.2 119.1 %all-gather.2.cloned.1.call-start = ((), (), s32[]{:S(2)}) async-start(), calls=%async_computation.1 | async-start | bytes 14598144 | tf_op jit(solution)/shard_map/all_gather | solution.py:337
  10.3 384.9 %reduce-scatter.2.cloned.1.call-start = ((), (), s32[]{:S(2)}) async-start(), calls=%async_computation.2 | async-start | bytes 10948608 | tf_op jit(solution)/shard_map/reduce_scatter | solution.py:395
  10.4 8.9 %copy-start.26 = (f32[64]{0:T(128)S(1)}, f32[64]{0:T(128)}, u32[]{:S(2)}) copy-start(f32[64]{0:T(128)} %param.26) | copy-start | bytes 772
  10.4 10.3 %copy-start.27 = (f32[64]{0:T(128)S(1)}, f32[64]{0:T(128)}, u32[]{:S(2)}) copy-start(f32[64]{0:T(128)} %param.27) | copy-start | bytes 772
  10.4 10.3 %copy-start.28 = (f32[64]{0:T(128)S(1)}, f32[64]{0:T(128)}, u32[]{:S(2)}) copy-start(f32[64]{0:T(128)} %param.25) | copy-start | bytes 772
  11.4 28.7 %copy-start.2 = (bf16[512,768]{1,0:T(8,128)(2,1)}, bf16[512,768]{1,0:T(8,128)(2,1)S(1)}, u32[]{:S(2)}) copy-start(bf16[512,768]{1,0:T(8,128)(2,1)S(1)} %get-tuple-element.77) | copy-start | bytes 2359300
  11.4 27.4 %collective-permute-start = (bf16[512,768]{1,0:T(8,128)(2,1)}, bf16[512,768]{1,0:T(8,128)(2,1)S(1)}, u32[]{:S(2)}, u32[]{:S(2)}) collective-permute-start(bf16[512,768]{1,0:T(8,128)(2,1)} %get-tuple-element.76), channel_id=1, source_target_pairs={{0,1},{1,0},{2,3},{3,2},{4,5},{5,4},{6,7},{7,6},{8,9},{9,8},{10,11... | collective-permute-start | bytes 2359304 | tf_op jit(solution)/shard_map/ppermute | solution.py:320
  14.4 21.8 %collective-permute-start.2 = (s32[512]{0:T(512)S(1)}, s32[512]{0:T(512)S(1)}, u32[]{:S(2)}, u32[]{:S(2)}) collective-permute-start(s32[512]{0:T(512)S(1)} %bitcast.207), channel_id=1, source_target_pairs={{0,1},{1,0},{2,3},{3,2},{4,5},{5,4},{6,7},{7,6},{8,9},{9,8},{10,11... | collective-permute-start | bytes 6152 | tf_op jit(solution)/shard_map/ppermute | solution.py:320
  14.6 23.6 %collective-permute-start.1 = (f32[2688]{0:T(1024)S(1)}, f32[2688]{0:T(1024)S(1)}, u32[]{:S(2)}, u32[]{:S(2)}) collective-permute-start(f32[2688]{0:T(1024)S(1)} %constant_dynamic-update-slice_fusion), channel_id=1, source_target_pairs={{0,1},{1,0},{2,3},{3,2},{4,5},{5,4},{6,7},{7,6},{8,9},{9,8},{10,11... | collective-permute-start | bytes 32264 | tf_op jit(solution)/shard_map/ppermute | solution.py:349
  19.2 20.9 %copy-start.18 = (f32[768]{0:T(1024)S(1)}, f32[768]{0:T(1024)}, u32[]{:S(2)}) copy-start(f32[768]{0:T(1024)} %param.21) | copy-start | bytes 9220
  19.3 20.9 %copy-start.23 = (f32[768]{0:T(1024)S(1)}, f32[768]{0:T(1024)}, u32[]{:S(2)}) copy-start(f32[768]{0:T(1024)} %param.22) | copy-start | bytes 9220
  19.3 146.1 %collective-permute-start.3 = (bf16[512,768]{1,0:T(8,128)(2,1)}, bf16[512,768]{1,0:T(8,128)(2,1)}, u32[]{:S(2)}, u32[]{:S(2)}) collective-permute-start(bf16[512,768]{1,0:T(8,128)(2,1)} %get-tuple-element.75), channel_id=1, source_target_pairs={{0,1},{1,0},{2,3},{3,2},{4,5},{5,4},{6,7},{7,6},{8,9},{9,8},{10,11... | collective-permute-start | bytes 2359304 | tf_op jit(solution)/shard_map/ppermute | solution.py:320
  38.9 4.4 %copy-start.8 = (bf16[512,768]{1,0:T(8,128)(2,1)}, bf16[512,768]{1,0:T(8,128)(2,1)S(1)}, u32[]{:S(2)}) copy-start(bf16[512,768]{1,0:T(8,128)(2,1)S(1)} %collective-permute-done) | copy-start | bytes 2359300
  152.2 2.5 copy-start.3
  152.2 2.5 copy-start.9
  152.2 2.5 copy-start.17
  152.2 2.5 copy-start.29
  154.7 5.2 %copy-start.6 = (bf16[1536,4608]{1,0:T(8,128)(2,1)S(1)}, bf16[1536,4608]{1,0:T(8,128)(2,1)}, u32[]{:S(2)}) copy-start(bf16[1536,4608]{1,0:T(8,128)(2,1)} %all-gather.2.cloned.1.call-done) | copy-start | bytes 42467332
  159.9 5.4 %copy-start.14 = (bf16[512,768]{1,0:T(8,128)(2,1)S(1)}, bf16[512,768]{1,0:T(8,128)(2,1)}, u32[]{:S(2)}) copy-start(bf16[512,768]{1,0:T(8,128)(2,1)} %get-tuple-element.74) | copy-start | bytes 2359300
  206.6 2.0 copy-start.12
  215.3 1.9 copy-start.31
  226.9 52.5 %copy-start.16 = (bf16[1024,768]{1,0:T(8,128)(2,1)S(1)}, bf16[1024,768]{1,0:T(8,128)(2,1)}, u32[]{:S(2)}) copy-start(bf16[1024,768]{1,0:T(8,128)(2,1)} %fusion.18.x_ref) | copy-start | bytes 4718596
  279.4 4.1 %copy-start.13 = (bf16[2,1024,1152]{2,1,0:T(8,128)(2,1)S(1)}, bf16[2,1024,1152]{2,1,0:T(8,128)(2,1)}, u32[]{:S(2)}) copy-start(bf16[2,1024,1152]{2,1,0:T(8,128)(2,1)} %get-tuple-element.43) | copy-start | bytes 14155780
  286.1 2.4 copy-start.7
  287.6 11.9 %collective-permute-start.6 = (bf16[2,8,48,1152]{3,2,1,0:T(8,128)(2,1)}, bf16[2,8,48,1152]{3,2,1,0:T(8,128)(2,1)}, u32[]{:S(2)}, u32[]{:S(2)}) collective-permute-start(bf16[2,8,48,1152]{3,2,1,0:T(8,128)(2,1)} %dynamic-slice_bitcast_fusion), channel_id=1, source_target_pairs={{0,2},{2,0},{4,6},{6,4},{8,10},{10,8},{12,14},{14,12},{16,18},{18,... | collective-permute-start | bytes 5308424 | tf_op jit(solution)/shard_map/ppermute | solution.py:177
  289.2 3.9 copy-start.4
  289.2 3.9 copy-start.10
  299.4 4.2 %copy-start.1 = (f32[1024,768]{1,0:T(8,128)S(1)}, f32[1024,768]{1,0:T(8,128)}, u32[]{:S(2)}) copy-start(f32[1024,768]{1,0:T(8,128)} %copy-done) | copy-start | bytes 9437188
  299.5 4.2 %copy-start.5 = (bf16[512,768]{1,0:T(8,128)(2,1)S(1)}, bf16[512,768]{1,0:T(8,128)(2,1)}, u32[]{:S(2)}) copy-start(bf16[512,768]{1,0:T(8,128)(2,1)} %copy-done.2) | copy-start | bytes 2359300
  299.5 4.2 %copy-start.11 = (bf16[512,768]{1,0:T(8,128)(2,1)S(1)}, bf16[512,768]{1,0:T(8,128)(2,1)}, u32[]{:S(2)}) copy-start(bf16[512,768]{1,0:T(8,128)(2,1)} %copy-done.8) | copy-start | bytes 2359300
  302.2 53.1 %collective-permute-start.8 = (bf16[8,48,1152]{2,1,0:T(8,128)(2,1)S(1)}, bf16[8,48,1152]{2,1,0:T(8,128)(2,1)S(1)}, u32[]{:S(2)}, u32[]{:S(2)}) collective-permute-start(bf16[8,48,1152]{2,1,0:T(8,128)(2,1)S(1)} %dynamic-slice_bitcast_fusion.1), channel_id=1, source_target_pairs={{0,1},{1,0},{2,3},{3,2},{4,5},{5,4},{6,7},{7,6},{8,9},{9,8},{10,11... | collective-permute-start | bytes 2654216 | tf_op jit(solution)/shard_map/ppermute | solution.py:444
  303.6 6.9 %copy-start.34 = (bf16[1024,1536]{1,0:T(8,128)(2,1)S(1)}, bf16[1024,1536]{1,0:T(8,128)(2,1)}, u32[]{:S(2)}) copy-start(bf16[1024,1536]{1,0:T(8,128)(2,1)} %get-tuple-element.38) | copy-start | bytes 9437188
  308.4 64.4 %collective-permute-start.5 = (bf16[512,768]{1,0:T(8,128)(2,1)S(1)}, bf16[512,768]{1,0:T(8,128)(2,1)S(1)}, u32[]{:S(2)}, u32[]{:S(2)}) collective-permute-start(bf16[512,768]{1,0:T(8,128)(2,1)S(1)} %fusion.52), channel_id=1, source_target_pairs={{0,1},{1,0},{2,3},{3,2},{4,5},{5,4},{6,7},{7,6},{8,9},{9,8},{10,11... | collective-permute-start | bytes 2359304 | tf_op jit(solution)/shard_map/ppermute | solution.py:324
  308.9 46.3 %collective-permute-start.7 = (f32[10176]{0:T(1024)S(1)}, f32[10176]{0:T(1024)S(1)}, u32[]{:S(2)}, u32[]{:S(2)}) collective-permute-start(f32[10176]{0:T(1024)S(1)} %concatenate.104), channel_id=1, source_target_pairs={{0,1},{1,0},{2,3},{3,2},{4,5},{5,4},{6,7},{7,6},{8,9},{9,8},{10,11... | collective-permute-start | bytes 122120 | tf_op jit(solution)/shard_map/ppermute | solution.py:445
  314.9 42.2 %copy-start.30 = (f32[768]{0:T(1024)S(1)}, f32[768]{0:T(1024)}, u32[]{:S(2)}) copy-start(f32[768]{0:T(1024)} %param.35) | copy-start | bytes 9220
  314.9 42.2 %copy-start.32 = (bf16[1024,1536]{1,0:T(8,128)(2,1)S(1)}, bf16[1024,1536]{1,0:T(8,128)(2,1)}, u32[]{:S(2)}) copy-start(bf16[1024,1536]{1,0:T(8,128)(2,1)} %get-tuple-element.39) | copy-start | bytes 9437188
  355.6 14.3 %collective-permute-start.10 = (bf16[1,4,48,1152]{3,2,1,0:T(8,128)(2,1)S(1)}, bf16[1,4,48,1152]{3,2,1,0:T(8,128)(2,1)S(1)}, u32[]{:S(2)}, u32[]{:S(2)}) collective-permute-start(bf16[1,4,48,1152]{3,2,1,0:T(8,128)(2,1)S(1)} %dynamic-slice_bitcast_fusion.7), channel_id=1, source_target_pairs={{0,4},{2,6},{4,0},{6,2},{8,12},{10,14},{12,8},{14,10},{16,20},{18,... | collective-permute-start | bytes 1327112 | tf_op jit(solution)/shard_map/ppermute | solution.py:177
  361.7 1.3 collective-permute-start.9
  361.9 25.9 %collective-permute-start.4 = (bf16[512,768]{1,0:T(8,128)(2,1)S(1)}, bf16[512,768]{1,0:T(8,128)(2,1)S(1)}, u32[]{:S(2)}, u32[]{:S(2)}) collective-permute-start(bf16[512,768]{1,0:T(8,128)(2,1)S(1)} %get-tuple-element.73), channel_id=1, source_target_pairs={{0,1},{1,0},{2,3},{3,2},{4,5},{5,4},{6,7},{7,6},{8,9},{9,8},{10,11... | collective-permute-start | bytes 2359304 | tf_op jit(solution)/shard_map/ppermute | solution.py:324
  370.0 9.5 %collective-permute-start.12 = (bf16[1,2,48,1152]{3,2,1,0:T(8,128)(2,1)S(1)}, bf16[1,2,48,1152]{3,2,1,0:T(8,128)(2,1)S(1)}, u32[]{:S(2)}, u32[]{:S(2)}) collective-permute-start(bf16[1,2,48,1152]{3,2,1,0:T(8,128)(2,1)S(1)} %dynamic-slice_bitcast_fusion.8), channel_id=1, source_target_pairs={{0,8},{2,10},{4,12},{6,14},{8,0},{10,2},{12,4},{14,6},{16,24},{18,... | collective-permute-start | bytes 663560 | tf_op jit(solution)/shard_map/ppermute | solution.py:177
  371.4 4.0 collective-permute-start.11
  379.7 7.9 %collective-permute-start.14 = (bf16[1,1,48,1152]{3,2,1,0:T(8,128)(2,1)S(1)}, bf16[1,1,48,1152]{3,2,1,0:T(8,128)(2,1)S(1)}, u32[]{:S(2)}, u32[]{:S(2)}) collective-permute-start(bf16[1,1,48,1152]{3,2,1,0:T(8,128)(2,1)S(1)} %constant_dynamic-slice_fusion), channel_id=1, source_target_pairs={{0,16},{2,18},{4,20},{6,22},{8,24},{10,26},{12,28},{14,30},{16,0},... | collective-permute-start | bytes 331784 | tf_op jit(solution)/shard_map/ppermute | solution.py:177
  381.9 5.7 %collective-permute-start.13 = (f32[10176]{0:T(1024)S(1)}, f32[10176]{0:T(1024)S(1)}, u32[]{:S(2)}, u32[]{:S(2)}) collective-permute-start(f32[10176]{0:T(1024)S(1)} %add.280), channel_id=1, source_target_pairs={{0,8},{2,10},{4,12},{6,14},{8,0},{10,2},{12,4},{14,6},{16,24},{18,... | collective-permute-start | bytes 122120 | tf_op jit(solution)/shard_map/ppermute | solution.py:182
  387.6 5.0 %collective-permute-start.15 = (f32[10176]{0:T(1024)S(1)}, f32[10176]{0:T(1024)S(1)}, u32[]{:S(2)}, u32[]{:S(2)}) collective-permute-start(f32[10176]{0:T(1024)S(1)} %add.285), channel_id=1, source_target_pairs={{0,16},{2,18},{4,20},{6,22},{8,24},{10,26},{12,28},{14,30},{16,0},... | collective-permute-start | bytes 122120 | tf_op jit(solution)/shard_map/ppermute | solution.py:182
  (5 other events, 8.2 us)
Sparse Core Ops, SparseCore 0:
  11.5 114.7 all-gather.1
  226.9 152.6 reduce-scatter.1
